TPU v7x, 256 devices: a whole 4x4x8 slice. The times are simulated.
256 devices in a mesh: gx: 8 (over x, core), gy: 8 (over z), gz: 4 (over y).
Axes of the slice: x: 4, y: 4, z: 8, core: 2. Of those that a mesh axis runs over, the one named last changes fastest.
Arguments:
- pair_list: int32 [8192, 2], P(('gx', 'gy', 'gz')), may hold values from 0 to 63, all different within a row; in each aligned block of 32 rows (0 to 31, 32 to 63, ...) at most 2 rows name the same one
- rank_bucket: int32 [8192], P(('gx', 'gy', 'gz')), may hold values from 0 to 2
- amplitudes: bfloat16 [8192, 36864], P(('gx', 'gy', 'gz')), may hold values from -0.4375 to 0.4375
- intersects: bfloat16 [8192, 36864], P(('gx', 'gy', 'gz')), may hold values from -0.4375 to 0.4375
- integrals: bfloat16 [8192, 36864], P(('gx', 'gy', 'gz')), may hold values from -6 to 6
- exchange_blocks: bfloat16 [64, 36864], P(('gx', 'gy')), may hold values from -0.4375 to 0.4375
Outputs:
- residuals: bfloat16 [8192, 36864], P(('gx', 'gy', 'gz'))
Inputs may be any that keep to these rules, and one draw needn't show every extreme that they name: `pair_list`: each row names two different occupied orbitals; within the rows of one device no orbital is named more than 2 times, a bound that some block reaches on some devices. `rank_bucket`: bucket b keeps the leading (b + 1) * 64 PNOs.
All inputs are finite; a program needn't handle non-finite values.
Results may differ from a plain program's by a relative error of at most 0.013.
Values may be sent and summed in bfloat16 or wider, within the bound.
A program may use at most 128 MiB of HBM per device.

v0:
```python
import jax
import jax.numpy as jnp
from jax import lax
from jax.sharding import Mesh
from jax.sharding import PartitionSpec as P

RSTEP = 64
R = 192
GX = ("gx_0", "gx_1")
GX_GY = ("gx_0", "gx_1", "gy")
GX_GY_GZ = ("gx_0", "gx_1", "gy", "gz")


def own_block(blocks, axes, turns):
    shape = [lax.axis_size(a) for a in axes]
    blocks = blocks.reshape(*shape, *blocks.shape[1:])
    blocks = blocks.transpose(*turns, *range(len(axes), blocks.ndim))
    blocks = blocks.reshape(-1, *blocks.shape[len(axes) :])
    for k in turns:
        blocks = lax.psum_scatter(blocks, axes[k], scatter_dimension=0, tiled=True)
    return blocks[0]


def cut_along(array, dim, length):
    shape = array.shape
    blocks = array.reshape(*shape[:dim], length, shape[dim] // length, *shape[dim + 1 :])
    return jnp.moveaxis(blocks, dim, 0)


def sum_by_axis(array, axes, turns, dim):
    length = lax.axis_size(axes)
    return own_block(cut_along(array, dim, length), axes, turns)


def sent_to_all(array, axis):
    copies = jnp.broadcast_to(array, (lax.axis_size(axis), *array.shape))
    return lax.all_to_all(copies, axis, split_axis=0, concat_axis=0, tiled=True)


def of_everyone(array, axis):
    return sent_to_all(array, axis).sum(axis=0)


def side_by_side(arrays, axis, dim, along):
    both = jnp.concatenate(arrays, axis=along)
    whole, at, gathered = (lax.all_gather(both, axis, axis=dim, tiled=True), 0, [])
    for a in arrays:
        gathered.append(lax.slice_in_dim(whole, at, at + a.shape[along], axis=along))
        at += a.shape[along]
    return tuple(gathered)


def body(pair_list, rank_bucket, amplitudes, intersects, integrals, exchange_blocks):
    pair_rows = amplitudes.shape[0]
    rank_width = R
    owned_rows = exchange_blocks.shape[0]
    amplitudes = amplitudes.reshape(pair_rows, rank_width, rank_width)
    intersects = intersects.reshape(pair_rows, rank_width, rank_width)
    integrals = integrals.reshape(pair_rows, rank_width, rank_width)
    exchange_blocks = exchange_blocks.reshape(owned_rows, rank_width, rank_width)
    groups_x, groups_y = (lax.axis_size(GX), lax.axis_size("gy"))
    group_total = groups_x * groups_y
    occupied = owned_rows * group_total
    row_index = lax.broadcasted_iota(jnp.int32, (rank_width, rank_width), 0)
    col_index = lax.broadcasted_iota(jnp.int32, (rank_width, rank_width), 1)
    pair_rank = (rank_bucket + 1) * RSTEP
    inside = (row_index[None] < pair_rank[:, None, None]) & (
        col_index[None] < pair_rank[:, None, None]
    )
    masked = jnp.where(inside, amplitudes, jnp.zeros_like(amplitudes))
    half_projected = jnp.einsum(
        "pab,pbc->pac", intersects, masked, preferred_element_type=jnp.float32
    ).astype(jnp.bfloat16)
    projected = jnp.einsum(
        "pab,pcb->pac", half_projected, intersects, preferred_element_type=jnp.float32
    ).astype(jnp.bfloat16)
    local_term = jnp.einsum("pab,pbc->pac", masked, integrals, preferred_element_type=jnp.float32)
    flat_projected = projected.reshape(pair_rows, rank_width * rank_width)
    end_counts = jnp.sum(
        (pair_list[None] == lax.broadcasted_iota(jnp.int32, (occupied, 1, 1), 0)).astype(jnp.int32),
        axis=2,
    ).astype(jnp.bfloat16)
    partial_sum = sum_by_axis(
        jnp.dot(end_counts, flat_projected, preferred_element_type=jnp.float32), GX_GY, (1, 0, 2), 0
    ).reshape(owned_rows, rank_width, rank_width)
    domain = of_everyone(partial_sum, "gz")
    coupled = jnp.einsum(
        "oab,obc->oac",
        domain.astype(jnp.bfloat16),
        exchange_blocks,
        preferred_element_type=jnp.float32,
    ).astype(jnp.bfloat16)
    every_coupled, every_block = side_by_side((coupled, exchange_blocks), GX_GY, 0, 1)
    picked_blocks = every_block[pair_list]
    picked_coupled = every_coupled[pair_list]
    own_term = jnp.einsum(
        "pab,pebc->peac", projected, picked_blocks, preferred_element_type=jnp.float32
    ).astype(jnp.bfloat16)
    answers = (picked_coupled.astype(jnp.float32) - own_term.astype(jnp.float32)).astype(
        jnp.bfloat16
    )
    combined = (answers[:, 0].astype(jnp.float32) + answers[:, 1].astype(jnp.float32)).astype(
        jnp.bfloat16
    )
    half_back = jnp.einsum(
        "pba,pbc->pac", intersects, combined, preferred_element_type=jnp.float32
    ).astype(jnp.bfloat16)
    back_projected = jnp.einsum(
        "pab,pbc->pac", half_back, intersects, preferred_element_type=jnp.float32
    )
    residual_sum = integrals.astype(jnp.float32) + local_term + back_projected
    result = jnp.where(inside, residual_sum, jnp.zeros_like(residual_sum)).astype(jnp.bfloat16)
    return result.reshape(pair_rows, rank_width * rank_width)


def solution(mesh):
    torus = Mesh(
        mesh.devices.reshape(4, 2, mesh.shape["gy"], mesh.shape["gz"]), ("gx_0", "gx_1", "gy", "gz")
    )
    return jax.shard_map(
        body,
        mesh=torus,
        in_specs=(
            P(GX_GY_GZ, None),
            P(GX_GY_GZ),
            P(GX_GY_GZ, None),
            P(GX_GY_GZ, None),
            P(GX_GY_GZ, None),
            P(GX_GY, None),
        ),
        out_specs=P(GX_GY_GZ, None),
        check_vma=False,
    )
```

profile of v0, /device:TPU:1, one launch (start us, length us, event | category | flops | bytes accessed | tf_op | source)
XLA Modules:
  0.0 363.4 jit_solution(6201070427340524937)
XLA Ops:
  6.5 6.1 %reshape.57 = bf16[32,192,192]{2,1,0:T(8,128)(2,1)} reshape(bf16[32,36864]{1,0:T(8,128)(2,1)} %param.8) | data formatting | bytes 4718592 | tf_op jit(solution)/shard_map/reshape | solution.py:57
  12.7 5.0 %reshape.58 = bf16[32,192,192]{2,1,0:T(8,128)(2,1)S(1)} reshape(bf16[32,36864]{1,0:T(8,128)(2,1)} %param.9) | data formatting | bytes 4718592 | tf_op jit(solution)/shard_map/reshape | solution.py:58
  17.6 6.9 %fusion.20 = bf16[32,192,192]{2,1,0:T(8,128)(2,1)} fusion(bf16[32,192,192]{2,1,0:T(8,128)(2,1)S(1)} %reshape.58, bf16[32,192,192]{2,1,0:T(8,128)(2,1)} %reshape.57, s32[32]{0:T(128)S(1)} %add_multiply_fusion), kind=kOutput, calls=%fused_computation.22 | convolution fusion | flops 913047552 | bytes 7078016 | tf_op jit(solution)/shard_map/pab,pcb->pac/dot_general | solution.py:74
  24.6 6.2 %reshape.85 = bf16[32,36864,1,1]{1,0,2,3:T(8,128)(2,1)} reshape(bf16[32,192,192]{2,1,0:T(8,128)(2,1)} %fusion.20) | data formatting | bytes 4718592 | tf_op jit(solution)/shard_map/reshape | solution.py:78
  31.0 3.0 convolution_bitcast_fusion
  34.0 4.2 %copy.30 = f32[2,4,8,1,36864]{4,2,1,0,3:T(8,128)} copy(f32[2,4,8,1,36864]{4,2,0,1,3:T(8,128)S(1)} %convolution_bitcast_fusion) | data formatting | bytes 18874368 | tf_op jit(solution)/shard_map/transpose | solution.py:17
  38.3 27.1 %reduce-scatter.4.cloned.1.call-done = f32[32,1,36864]{2,0,1:T(8,128)} async-done(((f32[64,1,36864]{2,0,1:T(8,128)}), f32[32,1,36864]{2,0,1:T(8,128)}) %reduce-scatter.4.cloned.1.call-update) | async-done | bytes 4718608 | tf_op jit(solution)/shard_map/reduce_scatter | solution.py:20
  65.4 56.9 %reduce-scatter.6.cloned.1.call-done = f32[8,1,36864]{2,0,1:T(8,128)} async-done(((f32[32,1,36864]{2,0,1:T(8,128)}), f32[8,1,36864]{2,0,1:T(8,128)}) %reduce-scatter.6.cloned.1.call-update) | async-done | bytes 1179664 | tf_op jit(solution)/shard_map/reduce_scatter | solution.py:20
  122.4 0.6 dynamic-slice
  123.0 73.8 %all-reduce.3.cloned.1.call-done = f32[8,1,36864]{2,0,1:T(8,128)} async-done(((f32[8,1,36864]{2,0,1:T(8,128)}), f32[8,1,36864]{2,0,1:T(8,128)}) %all-reduce.3.cloned.1.call-update) | async-done | bytes 1179664
  196.7 2.3 dynamic-slice_reduce_fusion
  199.1 0.9 broadcast_in_dim.9
  200.1 4.2 %all-to-all-start = ((f32[4,1,192,192]{3,2,1,0:T(8,128)}), f32[4,1,192,192]{3,2,1,0:T(8,128)}, u32[]{:S(2)}, u32[]{:S(2)}) async-start(f32[4,1,192,192]{3,2,1,0:T(8,128)} %broadcast_in_dim.9), calls=%async_computation.2 | async-start | bytes 1572864 | tf_op jit(solution)/shard_map/all_to_all | solution.py:37
  204.3 0.2 all-gather.2.cloned.1.call-start
  204.5 1.3 reduce.2
  205.8 0.1 reshape.61
  205.9 0.1 reshape.62
  206.0 0.1 copy.31
  206.1 6.5 %all-to-all-done = f32[4,1,192,192]{3,2,1,0:T(8,128)} async-done(((f32[4,1,192,192]{3,2,1,0:T(8,128)}), f32[4,1,192,192]{3,2,1,0:T(8,128)}, u32[]{:S(2)}, u32[]{:S(2)}) %all-to-all-start) | async-done | bytes 589856 | tf_op jit(solution)/shard_map/all_to_all | solution.py:37
  212.7 1.2 reduce_sum.19
  213.9 0.2 fusion.23
  214.1 0.8 pad_maximum_fusion
  215.0 0.1 reshape.66
  215.1 6.1 %reshape.56 = bf16[32,192,192]{2,1,0:T(8,128)(2,1)} reshape(bf16[32,36864]{1,0:T(8,128)(2,1)} %param.10) | data formatting | bytes 4718592 | tf_op jit(solution)/shard_map/reshape | solution.py:59
  221.2 81.1 %all-gather.2.cloned.1.call-done = bf16[64,384,192]{1,2,0:T(8,128)(2,1)} async-done(((bf16[1,384,192]{1,2,0:T(8,128)(2,1)}), bf16[64,384,192]{1,2,0:T(8,128)(2,1)}) %all-gather.2.cloned.1.call-update) | async-done | bytes 9437200 | tf_op jit(solution)/shard_map/all_gather | solution.py:46
  302.3 12.0 %fusion.31 = (bf16[64,192,192]{1,2,0:T(8,128)(2,1)}, bf16[64,192,192]{1,2,0:T(8,128)(2,1)}) fusion(bf16[64,384,192]{1,2,0:T(8,128)(2,1)} %all-gather.2.cloned.1.call-done), kind=kLoop, calls=%fused_computation.35 | loop fusion | bytes 18874368 | tf_op jit(solution)/shard_map/slice | solution.py:48
  314.3 6.4 %gather_fusion = bf16[64,192,192]{1,2,0:T(8,128)(2,1)} fusion(bf16[64,192,192]{1,2,0:T(8,128)(2,1)} %get-tuple-element.6, s32[1024]{0:T(1024)S(1)} %pad_clamp_fusion), kind=kCustom, calls=%fused_computation | custom fusion | bytes 9437440 | tf_op jit(solution)/shard_map/gather | solution.py:95
  320.7 6.4 %gather_fusion.1 = bf16[64,192,192]{1,2,0:T(8,128)(2,1)} fusion(bf16[64,192,192]{1,2,0:T(8,128)(2,1)} %get-tuple-element.5, s32[1024]{0:T(1024)S(1)} %pad_clamp_fusion), kind=kCustom, calls=%fused_computation.1 | custom fusion | bytes 9437440 | tf_op jit(solution)/shard_map/gather | solution.py:94
  327.1 10.1 %fusion = bf16[32,2,192,192]{2,3,1,0:T(8,128)(2,1)} fusion(bf16[32,2,192,192]{2,3,1,0:T(8,128)(2,1)} %bitcast.39, bf16[32,2,192,192]{2,3,1,0:T(8,128)(2,1)} %bitcast.40, bf16[32,192,192]{2,1,0:T(8,128)(2,1)} %fusion.20), kind=kOutput, calls=%fused_computation.4 | convolution fusion | flops 917766144 | bytes 16515072 | tf_op jit(solution)/shard_map/pab,pebc->peac/dot_general | solution.py:96
  337.2 7.5 %fusion.9 = f32[32,192,192]{2,1,0:T(8,128)} fusion(bf16[32,192,192]{2,1,0:T(8,128)(2,1)S(1)} %reshape.58, bf16[32,2,192,192]{2,3,1,0:T(8,128)(2,1)} %fusion), kind=kOutput, calls=%fused_computation.16 | convolution fusion | flops 911867904 | bytes 15728640 | tf_op jit(solution)/shard_map/pab,pbc->pac/dot_general | solution.py:108
  344.8 7.9 %select_convert_fusion = bf16[32,192,192]{2,1,0:T(8,128)(2,1)S(1)} fusion(f32[32,192,192]{2,1,0:T(8,128)} %fusion.9, bf16[32,192,192]{2,1,0:T(8,128)(2,1)} %reshape.56, s32[32]{0:T(128)S(1)} %add_multiply_fusion, bf16[32,192,192]{2,1,0:T(8,128)(2,1)} %reshape.57), kind=kOutput, calls=%fused_computation.5 | convolution fusion | flops 467140608 | bytes 11796608 | tf_op jit(solution)/shard_map/pab,pbc->pac/dot_general | solution.py:77
  352.6 4.2 %reshape.63 = bf16[32,36864]{1,0:T(8,128)(2,1)} reshape(bf16[32,192,192]{2,1,0:T(8,128)(2,1)S(1)} %select_convert_fusion) | data formatting | bytes 4718592 | tf_op jit(solution)/shard_map/reshape | solution.py:113
  (21 shorter events, 0.5 us)
Async XLA Ops:
  6.5 58.8 %reduce-scatter.4.cloned.1.call-start = ((), (), s32[]{:S(2)}) async-start(), calls=%async_computation.3 | async-start | bytes 14155776 | tf_op jit(solution)/shard_map/reduce_scatter | solution.py:20
  12.7 5.0 %copy-start.1 = (s32[32]{0:T(128)S(1)}, s32[32]{0:T(128)}, u32[]{:S(2)}) copy-start(s32[32]{0:T(128)} %param.7) | copy-start | bytes 388
  24.6 6.2 %copy-start = (s32[32,2]{0,1:T(2,128)S(1)}, s32[32,2]{0,1:T(2,128)}, u32[]{:S(2)}) copy-start(s32[32,2]{0,1:T(2,128)} %param.6) | copy-start | bytes 772
  38.3 84.1 %copy-start.2 = (u32[256]{0:T(256)S(1)}, u32[256]{0:T(256)}, u32[]{:S(2)}) copy-start(u32[256]{0:T(256)} %constant.21) | copy-start | bytes 3076
  38.3 84.1 %reduce-scatter.6.cloned.1.call-start = ((), (), s32[]{:S(2)}) async-start(), calls=%async_computation.4 | async-start | bytes 5898240 | tf_op jit(solution)/shard_map/reduce_scatter | solution.py:20
  65.4 131.3 %all-reduce.3.cloned.1.call-start = ((), (), s32[]{:S(2)}) async-start(), calls=%async_computation.6 | async-start | bytes 2359296
  200.1 12.6 %all-to-all-start = ((f32[4,1,192,192]{3,2,1,0:T(8,128)}), f32[4,1,192,192]{3,2,1,0:T(8,128)}, u32[]{:S(2)}, u32[]{:S(2)}) async-start(f32[4,1,192,192]{3,2,1,0:T(8,128)} %broadcast_in_dim.9), calls=%async_computation.2 | async-start | bytes 1572864 | tf_op jit(solution)/shard_map/all_to_all | solution.py:37
  204.3 98.1 %all-gather.2.cloned.1.call-start = ((), (), s32[]{:S(2)}) async-start(), calls=%async_computation.5 | async-start | bytes 9584640 | tf_op jit(solution)/shard_map/all_gather | solution.py:46
Sparse Core Ops, SparseCore 0:
  38.4 26.9 reduce-scatter.3
  67.9 54.3 reduce-scatter.5
  124.7 71.9 all-reduce.2
  215.0 87.2 all-gather.1
where the time goes:
time: 364 us; the launch traced here: 363 us
  waiting for transfers between devices  245 us (67%)
  local copies, waits for them, and re-layouts  61.2 us (17%)
  matrix products  35.7 us (10%)
  between operations  13.3 us (4%)
  starting transfers between devices  4.49 us (1%)
    reduce_scatter x2, waiting for transfers between devices, own_block(): blocks = lax.psum_scatter(blocks, axes[k], scatter_dimension=0, tiled=True)  83.9 us
    all_gather x1, waiting for transfers between devices, side_by_side(): lax.all_gather(both, axis, axis=dim, tiled=True)  81.1 us
    unnamed x5, waiting for transfers between devices  73.8 us
    slice x1, local copies, waits for them, and re-layouts, side_by_side(): lax.slice_in_dim(whole, at, at + a.shape[along], axis=along)  12 us
    dot_general x1, matrix products, body(): jnp.einsum('pab,pebc->peac', projected, picked_blocks, preferred_element_...  10.1 us
    dot_general x1, matrix products, body(): jnp.einsum('pab,pbc->pac', masked, integrals, preferred_element_type=jnp....  7.89 us
    dot_general x1, matrix products, body(): jnp.einsum('pab,pbc->pac', half_back, intersects, preferred_element_type=...  7.5 us
  transfers between devices with their start and end apart: 5, of which 5 were waited for; matrix products, arithmetic and copies ran while one was open for 2% of the time, Pallas kernels for 0%

commit v1 on v0

v1 whole, which is shorter than its diff:
```python
import functools

import jax
import jax.numpy as jnp
from jax import lax
from jax.experimental import pallas as pl
from jax.experimental.pallas import tpu as pltpu
from jax.sharding import Mesh
from jax.sharding import PartitionSpec as P

RSTEP = 64
R = 192
Q = 48
CH = 80
GX_GY = ("gx_0", "gx_1", "gy")
GX_GY_GZ = ("gx_0", "gx_1", "gy", "gz")
MESH = pl.DeviceIdType.MESH
BF = jnp.bfloat16
F32 = jnp.float32


def pack(v):
    right = jnp.concatenate([v[:, 128:192], jnp.zeros((Q, 64), F32)], axis=1)
    first = right[0:16] + pltpu.roll(right[16:32], 64, 1)
    return jnp.concatenate([v[:, 0:128], first, right[32:48]], axis=0)


def unpack(c):
    first = c[48:64]
    right = jnp.concatenate([first, pltpu.roll(first, 64, 1), c[64:80]], axis=0)
    return jnp.concatenate([c[0:48], right], axis=1)


def dot(a, b, ca, cb):
    return lax.dot_general(a, b, (((ca,), (cb,)), ((), ())), preferred_element_type=F32)


def masked_block(t, rank):
    row = lax.broadcasted_iota(jnp.int32, (R, R), 0)
    col = lax.broadcasted_iota(jnp.int32, (R, R), 1)
    inside = (row < rank) & (col < rank)
    return inside, jnp.where(inside, t.astype(F32), 0.0)


def project_kernel(pairs, ranks, s_ref, t_ref, p_ref, dom_ref):
    p = pl.program_id(0)

    @pl.when(p == 0)
    def _():
        @pl.loop(0, 16)
        def _(i):
            dom_ref[i] = jnp.zeros(dom_ref.shape[1:], BF)

    s = s_ref[0]
    _, m = masked_block(t_ref[0], (ranks[p] + 1) * RSTEP)
    half = dot(s, m.astype(BF), 1, 0).astype(BF)
    full = dot(half, s, 1, 1).astype(BF)
    p_ref[0] = full
    full = full.astype(F32)
    for q in range(4):
        quarter = pack(full[Q * q : Q * q + Q])
        for e in range(2):
            k = pairs[2 * p + e]
            at = dom_ref.at[k // 4, q, k % 4]
            at[...] = (at[...].astype(F32) + quarter).astype(BF)


def exchange_kernel(dom, x_ref, gc, gx, rc_a, rc_b, acc_a, acc_b, tr_a, rx_a, tr_b, rx_b, tr_c, rx_c, tr_d, rx_d, zb, zr, send_sem, recv_sem):
    x, c, z, y = (lax.axis_index(a) for a in GX_GY_GZ)
    barrier = pltpu.get_barrier_semaphore()
    peers = [{"gx_1": 1 - c}]
    peers += [{"gx_0": (x + d) % 4} for d in (1, 3)]
    peers += [{"gz": (y + d) % 4} for d in (1, 3)]
    peers += [{"gy": (z + d) % 8} for d in range(1, 8)]
    for who in peers:
        pl.semaphore_signal(barrier, inc=1, device_id=who, device_id_type=MESH)
    pl.semaphore_wait(barrier, len(peers))

    started = []

    def send(src, dst, who):
        i = len(started)
        copy = pltpu.make_async_remote_copy(
            src_ref=src, dst_ref=dst, send_sem=send_sem.at[i], recv_sem=recv_sem.at[i], device_id=who, device_id_type=MESH
        )
        copy.start()
        started.append(copy)
        return copy

    def core(src, dst):
        return send(src, dst, {"gx_1": 1 - c})

    def add2(dst, i, a, b):
        dst[...] = (a[...].astype(F32) + b[...].astype(F32)).astype(BF)

    def add_into(n1, n2, dst, src):
        @pl.loop(0, n1)
        def _(i):
            for j in range(n2):
                dst[i, j] = (dst[i, j].astype(F32) + src[i, j].astype(F32)).astype(BF)

    def gather(g):
        g7 = g.reshape(4, 2, 2, 4, 4, CH, 128)

        over = []

        def across(ref):
            over.append(core(ref, ref))

        def at_own():
            return g.at[(x * 2 + c) * 2 + z // 4, y, z % 4]

        zc = [send(at_own(), at_own(), {"gy": (z + d) % 8}) for d in range(1, 8)]
        yield
        for copy in zc:
            copy.wait_recv()

        def piece_a2(q):
            return g.at[(x * 2 + c) * 2, q]

        def piece_b2(xx):
            return g.at[(xx * 2 + c) * 2 + 1, y]

        def piece_a3(xx):
            return g.at[(xx * 2 + c) * 2]

        def piece_b3(q):
            return g7.at[:, c, 1, q]

        def rings(specs, forward):
            copies = []
            for axis, pos, piece, half, n in specs:
                own = piece(pos)
                up = send(own, own, {axis: (pos + 1) % 4})
                down = send(own, own, {axis: (pos + 3) % 4})
                copies.append((up, down))
            if forward:
                for axis, pos, piece, half, n in specs:
                    across(piece(pos))
            yield
            second = []
            for (axis, pos, piece, half, n), (up, down) in zip(specs, copies):
                up.wait_recv()
                got = piece((pos + 3) % 4)
                low = send(got.at[0:half], got.at[0:half], {axis: (pos + 1) % 4})
                if forward:
                    across(got)
                down.wait_recv()
                got = piece((pos + 1) % 4)
                high = send(got.at[half:n], got.at[half:n], {axis: (pos + 3) % 4})
                if forward:
                    across(got)
                second.append((low, high))
            yield
            for (axis, pos, piece, half, n), (low, high) in zip(specs, second):
                got = piece((pos + 2) % 4)
                low.wait_recv()
                if forward:
                    across(got.at[0:half])
                high.wait_recv()
                if forward:
                    across(got.at[half:n])

        yield from rings([("gz", y, piece_a2, 2, 4), ("gx_0", x, piece_b2, 2, 4)], False)
        yield from rings([("gx_0", x, piece_a3, 2, 4), ("gz", y, piece_b3, 2, 4)], True)
        yield
        for copy in over:
            copy.wait_recv()

    own = pack(x_ref[pl.ds(pl.multiple_of(Q * y, Q), Q), :].astype(F32)).astype(BF)
    gx[(x * 2 + c) * 2 + z // 4, y, z % 4] = own

    dom7 = dom.reshape(4, 2, 2, 4, 4, CH, 128)
    order = (2, 1, 3, 0)
    first = []
    for d in order:
        xx, q = (x + d) % 4, (y + d) % 4
        first.append(
            (
                xx,
                q,
                core(dom7.at[xx, 1 - c, 0], rc_a.at[xx]),
                core(dom7.at[:, 1 - c, 1, q], rc_b.at[q]),
            )
        )

    gather_x = gather(gx)
    next(gather_x)

    def ring_reduce(specs):
        state = []
        for axis, pos, acc, n, transit, arrived, ready in specs:
            h = n // 2
            up, down = {axis: (pos + 1) % 4}, {axis: (pos + 3) % 4}
            pu, pd, far = (pos + 1) % 4, (pos + 3) % 4, (pos + 2) % 4
            ready(2)
            t_up = send(acc.at[far, 0:h], transit.at[0], up)
            t_dn = send(acc.at[far, h:n], transit.at[1], down)
            state.append([up, down, pu, pd, t_up, t_dn])
        for (axis, pos, acc, n, transit, arrived, ready), st in zip(specs, state):
            h = n // 2
            up, down, pu, pd, t_up, t_dn = st
            ready(1)
            a = send(acc.at[pu, h:n], arrived.at[0, h:n], up)
            ready(3)
            b = send(acc.at[pd, 0:h], arrived.at[1, 0:h], down)
            st += [a, b]
        for (axis, pos, acc, n, transit, arrived, ready), st in zip(specs, state):
            ready(0)
        yield
        for (axis, pos, acc, n, transit, arrived, ready), st in zip(specs, state):
            h = n // 2
            up, down, pu, pd, t_up, t_dn, a, b = st
            t_up.wait_recv()
            add_half(acc.at[pu, 0:h], transit.at[0])
            e = send(acc.at[pu, 0:h], arrived.at[0, 0:h], up)
            t_dn.wait_recv()
            add_half(acc.at[pd, h:n], transit.at[1])
            f = send(acc.at[pd, h:n], arrived.at[1, h:n], down)
            st += [e, f]
        yield
        for (axis, pos, acc, n, transit, arrived, ready), st in zip(specs, state):
            for copy in st[6:10]:
                copy.wait_recv()

    def add_half(dst, src):
        if len(dst.shape) == 4:
            add_into(dst.shape[0], dst.shape[1], dst, src)
        else:
            for j in range(dst.shape[0]):
                dst[j] = (dst[j].astype(F32) + src[j].astype(F32)).astype(BF)

    def ready_a(d):
        xx, q, ca, cb = first[order.index(d)]
        ca.wait_recv()

        @pl.loop(0, 4)
        def _(i):
            for j in range(4):
                acc_a[xx, i, j] = (dom[(xx * 2 + c) * 2, i, j].astype(F32) + rc_a[xx, i, j].astype(F32)).astype(BF)

    def ready_b(d):
        xx, q, ca, cb = first[order.index(d)]
        cb.wait_recv()

        @pl.loop(0, 4)
        def _(i):
            for j in range(4):
                acc_b[q, i, j] = (dom[(i * 2 + c) * 2 + 1, q, j].astype(F32) + rc_b[q, i, j].astype(F32)).astype(BF)

    ring = ring_reduce(
        [("gx_0", x, acc_a, 4, tr_a, rx_a, ready_a), ("gz", y, acc_b, 4, tr_b, rx_b, ready_b)]
    )
    next(ring)
    next(gather_x)
    next(ring)
    next(gather_x)
    for _ in ring:
        pass

    @pl.loop(0, 4)
    def _(i):
        for j in range(4):
            for acc, pos, arrived in ((acc_a, x, rx_a), (acc_b, y, rx_b)):
                acc[pos, i, j] = (acc[pos, i, j].astype(F32) + arrived[0, i, j].astype(F32) + arrived[1, i, j].astype(F32)).astype(BF)

    def nothing(d):
        return None

    ring = ring_reduce(
        [("gz", y, acc_a.at[x], 4, tr_c, rx_c, nothing), ("gx_0", x, acc_b.at[y], 4, tr_d, rx_d, nothing)]
    )
    next(ring)
    next(gather_x)
    next(ring)
    for _ in ring:
        pass
    for j in range(4):
        zb[j] = (acc_a[x, y, j].astype(F32) + rx_c[0, j].astype(F32) + rx_c[1, j].astype(F32)).astype(BF)
        zb[4 + j] = (acc_b[y, x, j].astype(F32) + rx_d[0, j].astype(F32) + rx_d[1, j].astype(F32)).astype(BF)

    zc = [send(zb.at[(z + d) % 8], zr.at[d - 1], {"gy": (z + d) % 8}) for d in range(1, 8)]
    next(gather_x)
    for copy in zc:
        copy.wait_recv()
    total = zb[z].astype(F32)
    for d in range(7):
        total = total + zr[d].astype(F32)
    domain = unpack(total)[:, 0:R].astype(BF)
    coupled = dot(domain, x_ref[...], 1, 0)
    gc[(x * 2 + c) * 2 + z // 4, y, z % 4] = pack(coupled).astype(BF)

    for _ in gather(gc):
        pass
    for _ in gather_x:
        pass
    for copy in started:
        copy.wait_send()


def finish_kernel(pairs, ranks, s_ref, t_ref, v_ref, p_ref, gc, gx, o_ref):
    p = pl.program_id(0)
    k0, k1 = pairs[2 * p], pairs[2 * p + 1]

    def both(g):
        parts = [
            unpack(g[k0 // 4, q, k0 % 4].astype(F32) + g[k1 // 4, q, k1 % 4].astype(F32)) for q in range(4)
        ]
        return jnp.concatenate(parts, axis=0)

    inside, m = masked_block(t_ref[0], (ranks[p] + 1) * RSTEP)
    s, v = s_ref[0], v_ref[0]
    own = dot(p_ref[0], both(gx).astype(BF), 1, 0)
    combined = (both(gc) - own)[:, 0:R].astype(BF)
    half = dot(combined, s, 1, 0).astype(BF)
    back = dot(s, half, 0, 0)
    local = dot(m.astype(BF), v, 1, 0)
    o_ref[0] = jnp.where(inside, v.astype(F32) + local + back, 0.0).astype(BF)


def body(pair_list, rank_bucket, amplitudes, intersects, integrals, exchange_blocks):
    n = amplitudes.shape[0]
    t = amplitudes.reshape(n, R, R)
    s = intersects.reshape(n, R, R)
    v = integrals.reshape(n, R, R)
    xb = exchange_blocks.reshape(R, R)
    pairs = pair_list.reshape(2 * n)
    block = pl.BlockSpec((1, R, R), lambda p, *_: (p, 0, 0))
    gathered = (16, 4, 4, CH, 128)
    whole = pl.BlockSpec(gathered, lambda p, *_: (0, 0, 0, 0, 0))
    projected, dom = pl.pallas_call(
        project_kernel,
        grid_spec=pltpu.PrefetchScalarGridSpec(
            num_scalar_prefetch=2, grid=(n,), in_specs=[block, block], out_specs=[block, whole]
        ),
        out_shape=[jax.ShapeDtypeStruct((n, R, R), BF), jax.ShapeDtypeStruct(gathered, BF)],
        compiler_params=pltpu.CompilerParams(vmem_limit_bytes=40 * 2**20),
    )(pairs, rank_bucket, s, t)

    vm = pl.BlockSpec(memory_space=pltpu.VMEM)
    tail = (CH, 128)
    gc, gx = pl.pallas_call(
        exchange_kernel,
        in_specs=[vm, vm],
        out_specs=[vm, vm],
        out_shape=[jax.ShapeDtypeStruct(gathered, BF)] * 2,
        scratch_shapes=[
            pltpu.VMEM((4, 4, 4) + tail, BF),
            pltpu.VMEM((4, 4, 4) + tail, BF),
            pltpu.VMEM((4, 4, 4) + tail, BF),
            pltpu.VMEM((4, 4, 4) + tail, BF),
            pltpu.VMEM((2, 2, 4) + tail, BF),
            pltpu.VMEM((2, 4, 4) + tail, BF),
            pltpu.VMEM((2, 2, 4) + tail, BF),
            pltpu.VMEM((2, 4, 4) + tail, BF),
            pltpu.VMEM((2, 2) + tail, BF),
            pltpu.VMEM((2, 4) + tail, BF),
            pltpu.VMEM((2, 2) + tail, BF),
            pltpu.VMEM((2, 4) + tail, BF),
            pltpu.VMEM((8,) + tail, BF),
            pltpu.VMEM((7,) + tail, BF),
            pltpu.SemaphoreType.DMA((128,)),
            pltpu.SemaphoreType.DMA((128,)),
        ],
        compiler_params=pltpu.CompilerParams(collective_id=0, has_side_effects=True, vmem_limit_bytes=60 * 2**20),
    )(dom, xb)

    out = pl.pallas_call(
        finish_kernel,
        grid_spec=pltpu.PrefetchScalarGridSpec(
            num_scalar_prefetch=2,
            grid=(n,),
            in_specs=[block, block, block, block, whole, whole],
            out_specs=block,
        ),
        out_shape=jax.ShapeDtypeStruct((n, R, R), BF),
        compiler_params=pltpu.CompilerParams(vmem_limit_bytes=40 * 2**20),
    )(pairs, rank_bucket, s, t, v, projected, gc, gx)
    return out.reshape(n, R * R)


def solution(mesh):
    torus = Mesh(mesh.devices.reshape(4, 2, mesh.shape["gy"], mesh.shape["gz"]), GX_GY_GZ)
    return jax.shard_map(
        body,
        mesh=torus,
        in_specs=(
            P(GX_GY_GZ, None),
            P(GX_GY_GZ),
            P(GX_GY_GZ, None),
            P(GX_GY_GZ, None),
            P(GX_GY_GZ, None),
            P(GX_GY, None),
        ),
        out_specs=P(GX_GY_GZ, None),
        check_vma=False,
    )
```

time: 364 us -> 168 us (0.46)
  waiting for transfers between devices: 245 us -> 0 us
  Pallas kernels: 0 us -> 133 us
  matrix products: 35.7 us -> 0 us
  local copies, waits for them, and re-layouts: 61.2 us -> 33.4 us
  between operations: 13.3 us -> 0.08 us
  starting transfers between devices: 4.49 us -> 0 us
    pallas_call x0 -> x3, Pallas kernels: none -> 133 us  [the longest x1 87.6 us: body(): pl.pallas_call(exchange_kernel, in_specs=[vm, vm], out_specs=[vm, vm], ou...]
    reduce_scatter x2 -> x0, waiting for transfers between devices: 83.9 us -> none  [own_block(): blocks = lax.psum_scatter(blocks, axes[k], scatter_dimension=0, tiled=True)]
    all_gather x1 -> x0, waiting for transfers between devices: 81.1 us -> none  [side_by_side(): lax.all_gather(both, axis, axis=dim, tiled=True)]
    unnamed x5 -> x0, waiting for transfers between devices: 73.8 us -> none
    dot_general x6 -> x0, matrix products: 35.7 us -> none  [the longest x1 10.1 us: body(): jnp.einsum('pab,pebc->peac', projected, picked_blocks, preferred_element_...]
    gather x2 -> x0, local copies, waits for them, and re-layouts: 12.8 us -> none  [the longest x1 6.39 us: body(): picked_coupled = every_coupled[pair_list]]
    slice x1 -> x0, local copies, waits for them, and re-layouts: 12 us -> none  [side_by_side(): lax.slice_in_dim(whole, at, at + a.shape[along], axis=along)]
    all_to_all x1 -> x0, waiting for transfers between devices: 6.51 us -> none  [sent_to_all(): return lax.all_to_all(copies, axis, split_axis=0, concat_axis=0, tiled=True)]
  transfers between devices with their start and end apart: 5 -> 0, of which waited for: 5 -> 0; matrix products, arithmetic and copies ran while one was open for 2% -> 0% of each run, Pallas kernels for 0% -> 0%
where the time goes in v1:
time: 168 us; the launch traced here: 167 us
  Pallas kernels  133 us (79%)
  local copies, waits for them, and re-layouts  33.4 us (20%)
    pallas_call x1, Pallas kernels, body(): pl.pallas_call(exchange_kernel, in_specs=[vm, vm], out_specs=[vm, vm], ou...  87.6 us
    pallas_call x1, Pallas kernels, body(): pl.pallas_call(finish_kernel, grid_spec=pltpu.PrefetchScalarGridSpec(num_...  28.7 us
    pallas_call x1, Pallas kernels, body(): pl.pallas_call(project_kernel, grid_spec=pltpu.PrefetchScalarGridSpec(num...  16.6 us
    unnamed x17, local copies, waits for them, and re-layouts  9.07 us
    reshape x1, local copies, waits for them, and re-layouts, body(): v = integrals.reshape(n, R, R)  6.18 us
    reshape x1, local copies, waits for them, and re-layouts, body(): return out.reshape(n, R * R)  6.17 us
    reshape x1, local copies, waits for them, and re-layouts, body(): t = amplitudes.reshape(n, R, R)  6.15 us
    reshape x1, local copies, waits for them, and re-layouts, body(): s = intersects.reshape(n, R, R)  4.93 us

profile of v1, /device:TPU:1, one launch (start us, length us, event | category | flops | bytes accessed | tf_op | source)
XLA Modules:
  0.0 166.8 jit_solution(17445134093263755959)
XLA Ops:
  0.0 4.9 %reshape.19.s_ref = bf16[32,192,192]{2,1,0:T(8,128)(2,1)S(1)} reshape(bf16[32,36864]{1,0:T(8,128)(2,1)} %param.9) | data formatting | bytes 4718592 | tf_op jit(solution)/shard_map/reshape | solution.py:324
  4.9 0.0 copy-start.7
  5.0 0.0 copy-start.5
  5.0 6.1 %reshape.20.t_ref = bf16[32,192,192]{2,1,0:T(8,128)(2,1)} reshape(bf16[32,36864]{1,0:T(8,128)(2,1)} %param.8) | data formatting | bytes 4718592 | tf_op jit(solution)/shard_map/reshape | solution.py:323
  11.1 0.0 copy-done.7
  11.1 0.1 copy.8
  11.2 0.1 reshape.18.pairs
  11.3 0.0 copy-done.5
  11.3 0.0 copy-start
  11.3 1.9 %copy-done = bf16[32,192,192]{2,1,0:T(8,128)(2,1)S(1)} copy-done((bf16[32,192,192]{2,1,0:T(8,128)(2,1)S(1)}, bf16[32,192,192]{2,1,0:T(8,128)(2,1)}, u32[]{:S(2)}) %copy-start) | copy-done | bytes 2359320
  13.2 0.0 copy-start.6
  13.2 16.6 %shard_map.64 = (bf16[32,192,192]{2,1,0:T(8,128)(2,1)S(1)}, bf16[16,4,4,80,128]{4,3,2,1,0:T(8,128)(2,1)}) custom-call(s32[64]{0:T(128)S(1)} %reshape.18.pairs, s32[32]{0:T(128)S(1)} %copy-done.5, bf16[32,192,192]{2,1,0:T(8,128)(2,1)S(1)} %reshape.19.s_ref, bf16[32,192,192]{2,1,0:T(8,128)(2,1)S(1)} %copy-done), custom_call_target="tpu_custom_call" | custom-call | tf_op jit(solution)/shard_map/pallas_call | solution.py:331
  29.8 0.0 copy-start.4
  29.8 1.7 copy-done.4
  31.5 0.0 copy-done.6
  31.5 0.4 reduce
  31.9 0.8 reshape.22.x_ref
  32.7 87.6 %shard_map.65 = (bf16[16,4,4,80,128]{4,3,2,1,0:T(8,128)(2,1)}, bf16[16,4,4,80,128]{4,3,2,1,0:T(8,128)(2,1)}) custom-call(bf16[16,4,4,80,128]{4,3,2,1,0:T(8,128)(2,1)} %get-tuple-element.10.dom, bf16[192,192]{1,0:T(8,128)(2,1)} %reshape.22.x_ref), custom_call_target="tpu_custom_call" | custom-call | tf_op jit(solution)/shard_map/pallas_call | solution.py:342
  120.3 6.2 %reshape.21.v_ref = bf16[32,192,192]{2,1,0:T(8,128)(2,1)} reshape(bf16[32,36864]{1,0:T(8,128)(2,1)} %param.10) | data formatting | bytes 4718592 | tf_op jit(solution)/shard_map/reshape | solution.py:325
  126.5 0.0 copy-start.1
  126.5 1.9 %copy-done.1 = bf16[32,192,192]{2,1,0:T(8,128)(2,1)S(1)} copy-done((bf16[32,192,192]{2,1,0:T(8,128)(2,1)S(1)}, bf16[32,192,192]{2,1,0:T(8,128)(2,1)}, u32[]{:S(2)}) %copy-start.1) | copy-done | bytes 2359320
  128.4 0.0 copy-start.3
  128.4 1.9 %copy-done.3 = bf16[32,192,192]{2,1,0:T(8,128)(2,1)S(1)} copy-done((bf16[32,192,192]{2,1,0:T(8,128)(2,1)S(1)}, bf16[32,192,192]{2,1,0:T(8,128)(2,1)}, u32[]{:S(2)}) %copy-start.3) | copy-done | bytes 2359320
  130.3 28.7 %shard_map.66 = bf16[32,192,192]{2,1,0:T(8,128)(2,1)S(1)} custom-call(s32[64]{0:T(128)S(1)} %reshape.18.pairs, s32[32]{0:T(128)S(1)} %copy-done.5, bf16[32,192,192]{2,1,0:T(8,128)(2,1)S(1)} %reshape.19.s_ref, bf16[32,192,192]{2,1,0:T(8,128)(2,1)S(1)} %copy-done.1, bf16[32,192,192]{2,1,0:T(8,128)(2,1)S(1)} %copy-done.3, bf16[32,192,192]{2,1,0:T(8,128)(2,1)} %copy-done.4, ...), custom_call_target="tpu_custom_call" | custom-call | tf_op jit(solution)/shard_map/pallas_call | solution.py:368
  159.0 0.0 copy-start.2
  159.0 1.6 copy-done.2
  160.6 6.2 %reshape.23 = bf16[32,36864]{1,0:T(8,128)(2,1)} reshape(bf16[32,192,192]{2,1,0:T(8,128)(2,1)} %copy-done.2) | data formatting | bytes 4718592 | tf_op jit(solution)/shard_map/reshape | solution.py:379
Async XLA Ops:
  4.9 6.2 %copy-start.7 = (s32[32,2]{0,1:T(2,128)S(1)}, s32[32,2]{0,1:T(2,128)}, u32[]{:S(2)}) copy-start(s32[32,2]{0,1:T(2,128)} %param.6) | copy-start | bytes 772
  5.0 6.4 %copy-start.5 = (s32[32]{0:T(128)S(1)}, s32[32]{0:T(128)}, u32[]{:S(2)}) copy-start(s32[32]{0:T(128)} %ranks.3) | copy-start | bytes 388
  11.3 1.9 %copy-start = (bf16[32,192,192]{2,1,0:T(8,128)(2,1)S(1)}, bf16[32,192,192]{2,1,0:T(8,128)(2,1)}, u32[]{:S(2)}) copy-start(bf16[32,192,192]{2,1,0:T(8,128)(2,1)} %reshape.20.t_ref) | copy-start | bytes 7077892
  13.2 18.3 %copy-start.6 = (bf16[1,36864]{1,0:T(2,128)(2,1)S(1)}, bf16[1,36864]{1,0:T(2,128)(2,1)}, u32[]{:S(2)}) copy-start(bf16[1,36864]{1,0:T(2,128)(2,1)} %param.11) | copy-start | bytes 221188
  29.8 1.7 copy-start.4
  126.5 1.9 %copy-start.1 = (bf16[32,192,192]{2,1,0:T(8,128)(2,1)S(1)}, bf16[32,192,192]{2,1,0:T(8,128)(2,1)}, u32[]{:S(2)}) copy-start(bf16[32,192,192]{2,1,0:T(8,128)(2,1)} %reshape.20.t_ref) | copy-start | bytes 7077892
  128.4 1.9 %copy-start.3 = (bf16[32,192,192]{2,1,0:T(8,128)(2,1)S(1)}, bf16[32,192,192]{2,1,0:T(8,128)(2,1)}, u32[]{:S(2)}) copy-start(bf16[32,192,192]{2,1,0:T(8,128)(2,1)} %reshape.21.v_ref) | copy-start | bytes 7077892
  159.0 1.6 copy-start.2

commit v2 on v1

v2 whole, which is shorter than its diff:
```python
import jax
import jax.numpy as jnp
from jax import lax
from jax.experimental import pallas as pl
from jax.experimental.pallas import tpu as pltpu
from jax.sharding import Mesh
from jax.sharding import PartitionSpec as P

RSTEP = 64
R = 192
W = 256
Q = 48
CH = 72
LINES = R * R // 128
GX_GY = ("gx_0", "gx_1", "gy")
GX_GY_GZ = ("gx_0", "gx_1", "gy", "gz")
MESH = pl.DeviceIdType.MESH
BF = jnp.bfloat16
F32 = jnp.float32


def pack(v):
    right = v[:, 128:256]
    return jnp.concatenate([v[:, 0:128], right[0:24] + pltpu.roll(right[24:48], 64, 1)], axis=0)


def unpack(c):
    right = jnp.concatenate([c[48:72], pltpu.roll(c[48:72], 64, 1)], axis=0)
    return jnp.concatenate([c[0:48], right], axis=1)


def dot(a, b, ca=1, cb=0):
    return lax.dot_general(a, b, (((ca,), (cb,)), ((), ())), preferred_element_type=F32)


def low_lanes(n):
    return lax.broadcasted_iota(jnp.int32, (n, 128), 1) < 64


def even_odd(l0, l1, l2):
    low = low_lanes(l0.shape[0])
    t1, t2 = pltpu.roll(l1, 64, 1), pltpu.roll(l2, 64, 1)
    return (l0, jnp.where(low, l1, 0.0)), (jnp.where(low, t1, t2), jnp.where(low, t2, 0.0))


def kernel(
    inv, ranks, t_hbm, s_hbm, v_hbm, x_raw, o_hbm,
    s_raw, t_raw, v_raw, lines, xl, tmp, s_sq, m_sq, v_sq, x_sq, w_sq, st, pq, base, pp,
    gc, gx, sb_a, sb_b, rc_a, rc_b, acc_a, acc_b, tr_a, rx_a, tr_b, rx_b, tr_c, rx_c, tr_d, rx_d, zb, zr,
    pairs, load_sem, store_sem, send_sem, recv_sem,
):
    n = s_raw.shape[0]
    x, c, z, y = (lax.axis_index(a) for a in GX_GY_GZ)
    loads = []
    for i, (src, dst) in enumerate(((s_hbm, s_raw), (t_hbm, t_raw), (v_hbm, v_raw))):
        for g in range(n // 8):
            copy = pltpu.make_async_copy(src.at[8 * g : 8 * g + 8], dst.at[8 * g : 8 * g + 8], load_sem.at[i, g])
            copy.start()
            loads.append(copy)

    barrier = pltpu.get_barrier_semaphore()
    peers = [{"gx_1": 1 - c}]
    peers += [{"gx_0": (x + d) % 4} for d in (1, 3)]
    peers += [{"gz": (y + d) % 4} for d in (1, 3)]
    peers += [{"gy": (z + d) % 8} for d in range(1, 8)]
    for who in peers:
        pl.semaphore_signal(barrier, inc=1, device_id=who, device_id_type=MESH)

    started = []

    def send(src, dst, who):
        i = len(started)
        copy = pltpu.make_async_remote_copy(
            src_ref=src, dst_ref=dst, send_sem=send_sem.at[i], recv_sem=recv_sem.at[i], device_id=who, device_id_type=MESH
        )
        copy.start()
        started.append(copy)
        return copy

    def core(src, dst):
        return send(src, dst, {"gx_1": 1 - c})

    def gather(g):
        over = []

        def across(ref):
            over.append(core(ref, ref))

        own = g.at[x, c, z // 4, y, z % 4]
        zc = [send(own, own, {"gy": (z + d) % 8}) for d in range(1, 8)]
        yield
        for copy in zc:
            copy.wait_recv()

        def piece_a2(q):
            return g.at[x, c, 0, q]

        def piece_b2(xx):
            return g.at[xx, c, 1, y]

        def piece_a3(xx):
            return g.at[xx, c, 0]

        def piece_b3(q):
            return g.at[:, c, 1, q]

        def rings(specs, forward):
            copies = []
            for axis, pos, piece, half in specs:
                own = piece(pos)
                up = send(own, own, {axis: (pos + 1) % 4})
                down = send(own, own, {axis: (pos + 3) % 4})
                copies.append((up, down))
            if forward:
                for axis, pos, piece, half in specs:
                    across(piece(pos))
            yield
            second = []
            for (axis, pos, piece, half), (up, down) in zip(specs, copies):
                up.wait_recv()
                got = piece((pos + 3) % 4)
                low = send(got.at[0:half], got.at[0:half], {axis: (pos + 1) % 4})
                if forward:
                    across(got)
                down.wait_recv()
                got = piece((pos + 1) % 4)
                high = send(got.at[half:4], got.at[half:4], {axis: (pos + 3) % 4})
                if forward:
                    across(got)
                second.append((low, high))
            yield
            for (axis, pos, piece, half), (low, high) in zip(specs, second):
                got = piece((pos + 2) % 4)
                low.wait_recv()
                if forward:
                    across(got.at[0:half])
                high.wait_recv()
                if forward:
                    across(got.at[half:4])

        yield from rings([("gz", y, piece_a2, 2), ("gx_0", x, piece_b2, 2)], False)
        yield from rings([("gx_0", x, piece_a3, 2), ("gz", y, piece_b3, 2)], True)
        yield
        for copy in over:
            copy.wait_recv()

    @pl.loop(0, LINES // 8)
    def _(i):
        for u in range(8):
            xl[pl.ds(i * 8 + u, 1), :] = x_raw[0:1, pl.ds(pl.multiple_of((i * 8 + u) * 128, 128), 128)].astype(F32)

    even, odd = even_odd(*(xl[pl.ds(i, 96, stride=3), :] for i in range(3)))
    at = lax.broadcasted_iota(jnp.int32, (W, W), 1)
    to = jnp.where(at < 96, 2 * at, jnp.where(at < R, 2 * at - (R - 1), -1))
    turn = (lax.broadcasted_iota(jnp.int32, (W, W), 0) == to).astype(F32).astype(BF)
    for i, half in enumerate((even, odd)):
        x_sq[96 * i : 96 * i + 96, :] = dot(jnp.concatenate(half, axis=1).astype(BF), turn).astype(BF)
    x_sq[R:W, :] = jnp.zeros((W - R, W), BF)
    gx[x, c, z // 4, y, z % 4] = pack(
        x_sq[pl.ds(pl.multiple_of(Q * y, Q), Q), :].astype(F32)
    ).astype(BF)
    for i in range(2):
        w_sq[i, R:W, :] = jnp.zeros((W - R, W), BF)
        v_sq[i, R:W, :] = jnp.zeros((W - R, W), BF)
    pp[n] = jnp.zeros((4, CH, 128), BF)

    pl.semaphore_wait(barrier, len(peers))
    gather_x = gather(gx)
    next(gather_x)

    def to_lines(raw, g):
        @pl.loop(0, LINES // 12)
        def _(i):
            for u in range(12):
                at = i * 12 + u
                lines[pl.ds(pl.multiple_of(at * 8, 8), 8), :] = raw[
                    8 * g : 8 * g + 8, pl.ds(pl.multiple_of(at * 128, 128), 128)
                ].astype(F32)

    def halves(p):
        return even_odd(*(lines[pl.ds(8 * i + p, 96, stride=24), :] for i in range(3)))

    def natural(p, u):
        for i, half in enumerate(halves(p)):
            for j in range(2):
                tmp[u, j, pl.ds(i, 96, stride=2), :] = half[j]
        return square(u)

    def square(u):
        return jnp.concatenate([tmp[u, 0], tmp[u, 1]], axis=1)

    row = lax.broadcasted_iota(jnp.int32, (R, W), 0)
    col = lax.broadcasted_iota(jnp.int32, (R, W), 1)
    far = jnp.maximum(row, col)

    def project(g):
        loads[g].wait()
        to_lines(s_raw, g)

        @pl.loop(0, 8)
        def _(p):
            at = 8 * g + p
            for i, half in enumerate(halves(p)):
                s_sq[at, 96 * i : 96 * i + 96, :] = jnp.concatenate(half, axis=1).astype(BF)
            s_sq[at, R:W, :] = jnp.zeros((W - R, W), BF)

        loads[n // 8 + g].wait()
        to_lines(t_raw, g)

        @pl.loop(0, 4)
        def _(i):
            for u in range(2):
                p = 2 * i + u
                at = 8 * g + p
                m_sq[at, 0:R, :] = jnp.where(far < (ranks[at] + 1) * RSTEP, natural(p, u), 0.0).astype(BF)
                m_sq[at, R:W, :] = jnp.zeros((W - R, W), BF)
            for u in range(2):
                at = 8 * g + 2 * i + u
                half = dot(s_sq[at, 0:R, :], m_sq[at]).astype(BF)
                full = dot(half, s_sq[at], 1, 1).astype(BF)
                pq[at] = full
                full = full.astype(F32)
                for q in range(4):
                    pp[at, q] = pack(full[Q * q : Q * q + Q]).astype(BF)

    for g in range(n // 8):
        project(g)
        if g < 3:
            next(gather_x)

    def transposes(g):
        @pl.loop(0, 8)
        def _(p):
            st[8 * g + p] = s_sq[8 * g + p].T[0:R]

    def local(g):
        loads[2 * (n // 8) + g].wait()
        to_lines(v_raw, g)

        @pl.loop(0, 4)
        def _(i):
            for u in range(2):
                v_sq[u, 0:R, :] = natural(2 * i + u, u).astype(BF)
            for u in range(2):
                at = 8 * g + 2 * i + u
                base[at] = square(u) + dot(m_sq[at, 0:R, :], v_sq[u])

    def block(g, k, q):
        return g[k // 16, k // 8 % 2, k // 4 % 2, q, k % 4].astype(F32)

    def both(g, at):
        k0, k1 = pairs[2 * at], pairs[2 * at + 1]
        return jnp.concatenate(
            [unpack(block(g, k0, q) + block(g, k1, q)) for q in range(4)], axis=0
        )

    def own_terms(g):
        @pl.loop(0, 4)
        def _(i):
            for u in range(2):
                at = 8 * g + 2 * i + u
                w_sq[u, 0:R, :] = both(gx, at).astype(BF)
            for u in range(2):
                at = 8 * g + 2 * i + u
                pq[at] = dot(pq[at], w_sq[u]).astype(BF)

    early = [lambda g=g: local(g) for g in range(4)] + [lambda g=g: transposes(g) for g in range(4)]
    late = [lambda g=g: own_terms(g) for g in range(4)]

    def fill(work, count):
        for _ in range(count):
            if work:
                work.pop(0)()

    def ends(k):
        return pp[inv[2 * k]].astype(F32) + pp[inv[2 * k + 1]].astype(F32)

    order = (2, 1, 3, 0)
    first_a, first_b = [], []
    for d in order:
        xx = (x + d) % 4

        @pl.loop(0, 4)
        def _(j):
            k = (xx * 2 + 1 - c) * 8 + j
            sb_a[xx, :, j] = ends(k).astype(BF)
            sb_b[:, xx, j] = ends(k + 4).astype(BF)

        first_a.append(core(sb_a.at[xx], rc_a.at[xx]))
    for d in order:
        q = (y + d) % 4
        first_b.append(core(sb_b.at[q], rc_b.at[q]))

    for d in order:
        xx = (x + d) % 4

        @pl.loop(0, 4)
        def _(j):
            k = (xx * 2 + c) * 8 + j
            acc_a[xx, :, j] = ends(k).astype(BF)
            acc_b[:, xx, j] = ends(k + 4).astype(BF)

    def add_into(dst, src):
        if len(dst.shape) == 4:

            @pl.loop(0, dst.shape[0])
            def _(i):
                for j in range(dst.shape[1]):
                    dst[i, j] = (dst[i, j].astype(F32) + src[i, j].astype(F32)).astype(BF)
        else:
            for j in range(dst.shape[0]):
                dst[j] = (dst[j].astype(F32) + src[j].astype(F32)).astype(BF)

    def ready_a(d):
        first_a[order.index(d)].wait_recv()
        add_into(acc_a.at[(x + d) % 4], rc_a.at[(x + d) % 4])

    def ready_b(d):
        first_b[order.index(d)].wait_recv()
        add_into(acc_b.at[(y + d) % 4], rc_b.at[(y + d) % 4])

    def ring_reduce(specs):
        state = []
        for axis, pos, acc, transit, arrived, ready in specs:
            up, down = {axis: (pos + 1) % 4}, {axis: (pos + 3) % 4}
            far = (pos + 2) % 4
            ready(2)
            state.append([up, down, send(acc.at[far, 0:2], transit.at[0], up), send(acc.at[far, 2:4], transit.at[1], down)])
        for (axis, pos, acc, transit, arrived, ready), held in zip(specs, state):
            up, down = held[0:2]
            ready(1)
            held.append(send(acc.at[(pos + 1) % 4, 2:4], arrived.at[0, 2:4], up))
            ready(3)
            held.append(send(acc.at[(pos + 3) % 4, 0:2], arrived.at[1, 0:2], down))
        for spec in specs:
            spec[5](0)
        yield
        for (axis, pos, acc, transit, arrived, ready), held in zip(specs, state):
            up, down, t_up, t_down = held[0:4]
            t_up.wait_recv()
            add_into(acc.at[(pos + 1) % 4, 0:2], transit.at[0])
            held.append(send(acc.at[(pos + 1) % 4, 0:2], arrived.at[0, 0:2], up))
            t_down.wait_recv()
            add_into(acc.at[(pos + 3) % 4, 2:4], transit.at[1])
            held.append(send(acc.at[(pos + 3) % 4, 2:4], arrived.at[1, 2:4], down))
        yield
        for held in state:
            for copy in held[4:8]:
                copy.wait_recv()

    ring = ring_reduce([("gx_0", x, acc_a, tr_a, rx_a, ready_a), ("gz", y, acc_b, tr_b, rx_b, ready_b)])
    next(ring)
    next(gather_x)
    fill(early, 2)
    next(ring)
    next(gather_x)
    fill(early, 3)
    for _ in ring:
        pass

    @pl.loop(0, 4)
    def _(i):
        for j in range(4):
            for acc, pos, arrived in ((acc_a, x, rx_a), (acc_b, y, rx_b)):
                acc[pos, i, j] = (
                    acc[pos, i, j].astype(F32) + arrived[0, i, j].astype(F32) + arrived[1, i, j].astype(F32)
                ).astype(BF)

    def nothing(d):
        return None

    ring = ring_reduce(
        [("gz", y, acc_a.at[x], tr_c, rx_c, nothing), ("gx_0", x, acc_b.at[y], tr_d, rx_d, nothing)]
    )
    next(ring)
    fill(early, 2)
    next(ring)
    for _ in gather_x:
        pass
    fill(early, 1)
    for _ in ring:
        pass
    for j in range(4):
        zb[j] = (acc_a[x, y, j].astype(F32) + rx_c[0, j].astype(F32) + rx_c[1, j].astype(F32)).astype(BF)
        zb[4 + j] = (acc_b[y, x, j].astype(F32) + rx_d[0, j].astype(F32) + rx_d[1, j].astype(F32)).astype(BF)

    zc = [send(zb.at[(z + d) % 8], zr.at[d - 1], {"gy": (z + d) % 8}) for d in range(1, 8)]
    fill(late, 3)
    for copy in zc:
        copy.wait_recv()
    total = zb[z].astype(F32)
    for d in range(7):
        total = total + zr[d].astype(F32)
    domain = unpack(total).astype(BF)
    coupled = dot(domain, x_sq[...])
    gc[x, c, z // 4, y, z % 4] = pack(coupled).astype(BF)

    for _ in gather(gc):
        fill(late, 1)

    stores = []
    for g in range(n // 8):

        @pl.loop(0, 4)
        def _(i):
            for u in range(2):
                at = 8 * g + 2 * i + u
                combined = (both(gc, at) - pq[at].astype(F32)).astype(BF)
                w_sq[u, 0:R, :] = dot(combined, s_sq[at]).astype(BF)
            for u in range(2):
                at = 8 * g + 2 * i + u
                result = jnp.where(far < (ranks[at] + 1) * RSTEP, base[at] + dot(st[at], w_sq[u]), 0.0)
                tmp[u, 0] = result[:, 0:128]
                tmp[u, 1] = result[:, 128:256]
            for u in range(2):
                p = 2 * i + u
                low = low_lanes(96)
                el, er, ol, oh = (tmp[u, j, pl.ds(e, 96, stride=2), :] for e in range(2) for j in range(2))
                ol, oh = pltpu.roll(ol, 64, 1), pltpu.roll(oh, 64, 1)
                lines[pl.ds(p, 96, stride=24), :] = el
                lines[pl.ds(8 + p, 96, stride=24), :] = jnp.where(low, er, ol)
                lines[pl.ds(16 + p, 96, stride=24), :] = jnp.where(low, ol, oh)

        @pl.loop(0, LINES // 12)
        def _(i):
            for u in range(12):
                at = i * 12 + u
                s_raw[8 * g : 8 * g + 8, pl.ds(pl.multiple_of(at * 128, 128), 128)] = lines[
                    pl.ds(pl.multiple_of(at * 8, 8), 8), :
                ].astype(BF)

        copy = pltpu.make_async_copy(s_raw.at[8 * g : 8 * g + 8], o_hbm.at[8 * g : 8 * g + 8], store_sem.at[g])
        copy.start()
        stores.append(copy)
    for copy in stores:
        copy.wait()
    for copy in started:
        copy.wait_send()


def body(pair_list, rank_bucket, amplitudes, intersects, integrals, exchange_blocks):
    n = amplitudes.shape[0]
    named = (pair_list[None] == jnp.arange(64, dtype=jnp.int32)[:, None, None]).any(axis=2)
    number = jnp.arange(n, dtype=jnp.int32)[None, :]
    low = jnp.min(jnp.where(named, number, n), axis=1)
    high = jnp.max(jnp.where(named, number, -1), axis=1)
    inv = jnp.stack([low, jnp.where(high > low, high, n)], axis=1).reshape(128)

    smem = pl.BlockSpec(memory_space=pltpu.SMEM)
    hbm = pl.BlockSpec(memory_space=pl.ANY)
    vmem = pl.BlockSpec(memory_space=pltpu.VMEM)
    tail = (CH, 128)
    return pl.pallas_call(
        lambda inv, ranks, pairs, t, s, v, xr, o, *rest: kernel(inv, ranks, t, s, v, xr, o, *rest[:-4], pairs, *rest[-4:]),
        in_specs=[smem, smem, smem, hbm, hbm, hbm, vmem],
        out_specs=hbm,
        out_shape=jax.ShapeDtypeStruct((n, R * R), BF),
        scratch_shapes=[
            pltpu.VMEM((n, R * R), BF),
            pltpu.VMEM((n, R * R), BF),
            pltpu.VMEM((n, R * R), BF),
            pltpu.VMEM((LINES * 8, 128), F32),
            pltpu.VMEM((LINES, 128), F32),
            pltpu.VMEM((2, 2, R, 128), F32),
            pltpu.VMEM((n, W, W), BF),
            pltpu.VMEM((n, W, W), BF),
            pltpu.VMEM((2, W, W), BF),
            pltpu.VMEM((W, W), BF),
            pltpu.VMEM((2, W, W), BF),
            pltpu.VMEM((n, R, W), BF),
            pltpu.VMEM((n, R, W), BF),
            pltpu.VMEM((n, R, W), F32),
            pltpu.VMEM((n + 1, 4) + tail, BF),
            pltpu.VMEM((4, 2, 2, 4, 4) + tail, BF),
            pltpu.VMEM((4, 2, 2, 4, 4) + tail, BF),
            *[pltpu.VMEM((4, 4, 4) + tail, BF)] * 6,
            *[pltpu.VMEM((2, 2, 4) + tail, BF), pltpu.VMEM((2, 4, 4) + tail, BF)] * 2,
            *[pltpu.VMEM((2, 2) + tail, BF), pltpu.VMEM((2, 4) + tail, BF)] * 2,
            pltpu.VMEM((8,) + tail, BF),
            pltpu.VMEM((7,) + tail, BF),
            pltpu.SemaphoreType.DMA((3, n // 8)),
            pltpu.SemaphoreType.DMA((n // 8,)),
            pltpu.SemaphoreType.DMA((112,)),
            pltpu.SemaphoreType.DMA((112,)),
        ],
        compiler_params=pltpu.CompilerParams(collective_id=0, has_side_effects=True, vmem_limit_bytes=67043328),
    )(inv, rank_bucket, pair_list.reshape(2 * n), amplitudes, intersects, integrals, exchange_blocks)


def solution(mesh):
    torus = Mesh(mesh.devices.reshape(4, 2, mesh.shape["gy"], mesh.shape["gz"]), GX_GY_GZ)
    return jax.shard_map(
        body,
        mesh=torus,
        in_specs=(
            P(GX_GY_GZ, None),
            P(GX_GY_GZ),
            P(GX_GY_GZ, None),
            P(GX_GY_GZ, None),
            P(GX_GY_GZ, None),
            P(GX_GY, None),
        ),
        out_specs=P(GX_GY_GZ, None),
        check_vma=False,
    )
```

time: 168 us -> 110 us (0.65)
  Pallas kernels: 133 us -> 104 us
  local copies, waits for them, and re-layouts: 33.4 us -> 5.34 us
    pallas_call x3 -> x1, Pallas kernels: 133 us -> 104 us  [body(): pl.pallas_call(lambda inv, ranks, pairs, t, s, v, xr, o, *rest: kernel(in...]
    reshape x6 -> x2, local copies, waits for them, and re-layouts: 24.3 us -> 1.26 us  [the longest x1 0.65 us: body(): inv = jnp.stack([low, jnp.where(high > low, high, n)], axis=1).reshape(128)]
    unnamed x17 -> x2, local copies, waits for them, and re-layouts: 9.07 us -> 3.98 us
where the time goes in v2:
time: 110 us
  Pallas kernels  104 us (95%)
  local copies, waits for them, and re-layouts  5.34 us (5%)
    pallas_call x1, Pallas kernels, body(): pl.pallas_call(lambda inv, ranks, pairs, t, s, v, xr, o, *rest: kernel(in...  104 us
    unnamed x2, local copies, waits for them, and re-layouts  3.98 us

profile of v2, /device:TPU:1, one launch (start us, length us, event | category | flops | bytes accessed | tf_op | source)
XLA Modules:
  0.0 110.1 jit_solution(10794757910690366248)
XLA Ops:
  0.0 0.8 fusion
  0.8 0.8 copy.14
  1.6 0.6 reshape.22.pairs
  2.2 0.1 copy.13
  2.3 0.7 reshape.21.inv
  2.9 104.0 %shard_map.64 = bf16[32,36864]{1,0:T(8,128)(2,1)} custom-call(s32[128]{0:T(128)} %reshape.21.inv, s32[32]{0:T(128)} %ranks.1, s32[64]{0:T(128)} %reshape.22.pairs, bf16[32,36864]{1,0:T(8,128)(2,1)} %t.1, bf16[32,36864]{1,0:T(8,128)(2,1)} %s.1, bf16[32,36864]{1,0:T(8,128)(2,1)} %v.1, bf16[1,36864]{1,0:T(2,128)(2,1)} %xr.1), custom_call_target="tpu_custom_call" | custom-call | tf_op jit(solution)/shard_map/pallas_call | solution.py:453
  106.9 3.2 %copy.16 = bf16[32,36864]{1,0:T(8,128)(2,1)} copy(bf16[32,36864]{1,0:T(8,128)(2,1)} %shard_map.64) | data formatting | bytes 4718592
  (3 shorter events, 0.0 us)

commit v3 on v0

v3 whole, which is shorter than its diff:
```python
import itertools
import math

import jax
import jax.numpy as jnp
from jax import lax
from jax.experimental import pallas as pl
from jax.experimental.pallas import tpu as pltpu
from jax.sharding import Mesh
from jax.sharding import PartitionSpec as P

RSTEP = 64
R = 192
W = 256
Q = 48
CH = 72
LINES = R * R // 128
UNROLL = 4
OUT, INTO = 11, 96
GX_GY = ("gx_0", "gx_1", "gy")
GX_GY_GZ = ("gx_0", "gx_1", "gy", "gz")
MESH = pl.DeviceIdType.MESH
BF = jnp.bfloat16
F32 = jnp.float32


def pack(v):
    right = v[:, 128:256]
    return jnp.concatenate([v[:, 0:128], right[0:24] + pltpu.roll(right[24:48], 64, 1)], axis=0)


def unpack(c):
    right = jnp.concatenate([c[48:72], pltpu.roll(c[48:72], 64, 1)], axis=0)
    return jnp.concatenate([c[0:48], right], axis=1)


def dot(a, b, ca=1, cb=0):
    return lax.dot_general(a, b, (((ca,), (cb,)), ((), ())), preferred_element_type=F32)


def low_lanes(n):
    return lax.broadcasted_iota(jnp.int32, (n, 128), 1) < 64


def even_odd(l0, l1, l2):
    low = low_lanes(l0.shape[0])
    t1, t2 = pltpu.roll(l1, 64, 1), pltpu.roll(l2, 64, 1)
    return (l0, jnp.where(low, l1, 0.0)), (jnp.where(low, t1, t2), jnp.where(low, t2, 0.0))


def kernel(
    pairs_hbm, ranks_hbm, t_hbm, s_hbm, v_hbm, x_hbm, o_ref,
    s_raw, t_raw, v_raw, x_raw, lines, lines2, xl, tmp, s_sq, m_sq, v_sq, x_sq, w_sq, st, pq, base, pp,
    gc, gx, sb_a, sb_b, rc_a, rc_b, acc_a, acc_b, tr_a, rx_a, tr_b, rx_b, tr_c, rx_c, tr_d, rx_d, zb, zr,
    inv_v, inv, pairs, ranks, load_sem, store_sem, small_sem, send_sem, recv_sem,
):
    n = s_raw.shape[0]
    groups = n // 8
    x, c, z, y = (lax.axis_index(a) for a in GX_GY_GZ)
    barrier = pltpu.get_barrier_semaphore()
    peers = [{"gx_1": 1 - c}]
    peers += [{"gx_0": (x + d) % 4} for d in (1, 2, 3)]
    peers += [{"gz": (y + d) % 4} for d in (1, 3)]
    peers += [{"gy": (z + d) % 8} for d in range(1, 8)]
    for who in peers:
        pl.semaphore_signal(barrier, inc=1, device_id=who, device_id_type=MESH)

    small = []
    for i, (src, dst) in enumerate(((ranks_hbm, ranks), (pairs_hbm, pairs), (x_hbm, x_raw))):
        copy = pltpu.make_async_copy(src, dst, small_sem.at[i])
        copy.start()
        small.append(copy)
    loads = {}
    for i, g in [(i, g) for g in range(groups) for i in (0, 1)] + [(2, g) for g in range(groups)]:
        src, dst = ((s_hbm, s_raw), (t_hbm, t_raw), (v_hbm, v_raw))[i]
        copy = pltpu.make_async_copy(src.at[8 * g : 8 * g + 8], dst.at[8 * g : 8 * g + 8], load_sem.at[i, g])
        copy.start()
        loads[i, g] = copy

    leaving, arriving = {}, {}

    def slot(groups, name):
        groups.setdefault(name, [len(groups), 0])
        return groups[name]

    def send(src, dst, axis, at, out, into):
        size = math.prod(src.shape[:-2])
        for groups, name in ((leaving, out), (arriving, into)):
            slot(groups, name)[1] += size
        copy = pltpu.make_async_remote_copy(
            src_ref=src,
            dst_ref=dst,
            send_sem=send_sem.at[leaving[out][0]],
            recv_sem=recv_sem.at[arriving[into][0]],
            device_id={axis: at},
            device_id_type=MESH,
        )
        copy.start()

    def await_all(sem, size):
        for dims in itertools.product((4, 3, 2, 1), (2, 1), (2, 1), (4, 3, 2, 1), (4, 3, 2, 1)):
            if math.prod(dims) == size:
                ref = gc.at[tuple(slice(0, d) for d in dims)]
                break
        else:
            assert size == zr.shape[0]
            ref = zr
        pltpu.make_async_copy(ref, ref, sem).wait()

    def arrived(into):
        await_all(recv_sem.at[arriving[into][0]], arriving[into][1])

    def to_lines(raws, g):
        @pl.loop(0, LINES // 12)
        def _(i):
            for u in range(12):
                at = i * 12 + u
                for raw, to in zip(raws, (lines, lines2)):
                    to[pl.ds(pl.multiple_of(at * 8, 8), 8), :] = raw[
                        8 * g : 8 * g + 8, pl.ds(pl.multiple_of(at * 128, 128), 128)
                    ].astype(F32)

    def halves(src, p):
        return even_odd(*(src[pl.ds(8 * i + p, 96, stride=24), :] for i in range(3)))

    def natural(src, p, u):
        for i, half in enumerate(halves(src, p)):
            for j in range(2):
                tmp[u, j, pl.ds(i, 96, stride=2), :] = half[j]
        return square(u)

    def skewed(count, *stages):
        for step in range(count + len(stages) - 1):
            for i, stage in enumerate(stages):
                if 0 <= step - i < count:
                    stage(step - i)

    def square(u):
        return jnp.concatenate([tmp[u, 0], tmp[u, 1]], axis=1)

    row = lax.broadcasted_iota(jnp.int32, (R, W), 0)
    col = lax.broadcasted_iota(jnp.int32, (R, W), 1)
    far = jnp.maximum(row, col)

    def project(g):
        loads[0, g].wait()
        loads[1, g].wait()
        to_lines((s_raw, t_raw), g)

        @pl.loop(0, 8 // UNROLL)
        def _(i):
            half = {}

            def reshaped(u):
                p = UNROLL * i + u
                at = 8 * g + p
                for k, part in enumerate(halves(lines, p)):
                    s_sq[at, 96 * k : 96 * k + 96, :] = jnp.concatenate(part, axis=1).astype(BF)
                s_sq[at, R:W, :] = jnp.zeros((W - R, W), BF)
                m_sq[at, 0:R, :] = jnp.where(far < (ranks[at] + 1) * RSTEP, natural(lines2, p, u), 0.0).astype(BF)
                m_sq[at, R:W, :] = jnp.zeros((W - R, W), BF)

            def left(u):
                at = 8 * g + UNROLL * i + u
                half[u] = dot(s_sq[at, 0:R, :], m_sq[at]).astype(BF)

            def right(u):
                at = 8 * g + UNROLL * i + u
                full = dot(half.pop(u), s_sq[at], 1, 1).astype(BF)
                pq[at] = full
                full = full.astype(F32)
                for q in range(4):
                    pp[at, q] = pack(full[Q * q : Q * q + Q]).astype(BF)

            skewed(UNROLL, reshaped, left, right)

    small[0].wait()
    project(0)

    small[2].wait()

    @pl.loop(0, LINES // 8)
    def _(i):
        for u in range(8):
            xl[pl.ds(i * 8 + u, 1), :] = x_raw[0:1, pl.ds(pl.multiple_of((i * 8 + u) * 128, 128), 128)].astype(F32)

    even, odd = even_odd(*(xl[pl.ds(i, 96, stride=3), :] for i in range(3)))
    at = lax.broadcasted_iota(jnp.int32, (W, W), 1)
    to = jnp.where(at < 96, 2 * at, jnp.where(at < R, 2 * at - (R - 1), -1))
    turn = (lax.broadcasted_iota(jnp.int32, (W, W), 0) == to).astype(F32).astype(BF)
    for i, half in enumerate((even, odd)):
        x_sq[96 * i : 96 * i + 96, :] = dot(jnp.concatenate(half, axis=1).astype(BF), turn).astype(BF)
    x_sq[R:W, :] = jnp.zeros((W - R, W), BF)
    for q in range(4):
        gx[0, c, z, q] = pack(x_sq[Q * q : Q * q + Q, :].astype(F32)).astype(BF)
    for i in range(UNROLL):
        w_sq[i, R:W, :] = jnp.zeros((W - R, W), BF)
    for i in range(2):
        v_sq[i, R:W, :] = jnp.zeros((W - R, W), BF)
    pp[n] = jnp.zeros((4, CH, 128), BF)

    small[1].wait()
    lane = lax.broadcasted_iota(jnp.int32, (1, 128), 1)
    low = jnp.full((1, 128), n, jnp.int32)
    high = low
    for p in range(n):
        named = (lane == pairs[0, p]) | (lane == pairs[1, p])
        high = jnp.where(named & (low < n), p, high)
        low = jnp.where(named & (low == n), p, low)
    inv_v[0:1, :] = low
    inv_v[1:2, :] = high
    to_inv = pltpu.make_async_copy(inv_v, inv, small_sem.at[3])
    to_inv.start()

    pl.semaphore_wait(barrier, len(peers))

    def gather_blocks():
        pieces = ((slice(0, 1),) * 2, (slice(1, 2), slice(2, 3)), (slice(3, 4),) * 2)

        def ref(i, d):
            return gx.at[pieces[i][0].start : pieces[i][1].stop, c, (z + d) % 8]

        def hop(i, step):
            if step > 1:
                arrived(("xu", i, step - 1))
            up = ref(i, 9 - step)
            if step == 4:
                up = gx.at[pieces[i][0], c, (z + 5) % 8]
                up = up if i == 1 else up.at[:, 0:2]
            into = ("x4", i) if step == 4 else ("xu", i, step)
            send(up, up, "gy", (z + 1) % 8, "x4" if step == 4 else "xz", into)
            if step > 1:
                arrived(("xd", i, step - 1))
            down = ref(i, step - 1)
            if step == 4:
                down = gx.at[pieces[i][1], c, (z + 3) % 8]
                down = down if i == 1 else down.at[:, 2:4]
            into = ("x4", i) if step == 4 else ("xd", i, step)
            send(down, down, "gy", (z + 7) % 8, "x4" if step == 4 else "xz", into)
            if i == 2:
                for d in {(9 - step) % 8, step - 1}:
                    across_x(d)

        def across_x(d):
            send(gx.at[:, c, (z + d) % 8], gx.at[:, c, (z + d) % 8], "gx_1", 1 - c, "xc", "xc")

        own = gx.at[0, c, z]
        send(own, gx.at[2, c, z], "gx_0", (x + 1) % 4, "xx", "x-")
        send(own, gx.at[1, c, z], "gx_0", (x + 3) % 4, "xx", "x+")
        hop(0, 1)
        yield
        hop(0, 2)
        arrived("x-")
        send(gx.at[2, c, z, 0:2], gx.at[3, c, z, 0:2], "gx_0", (x + 1) % 4, "z", "x2")
        arrived("x+")
        send(gx.at[1, c, z, 2:4], gx.at[3, c, z, 2:4], "gx_0", (x + 3) % 4, "z", "x2")
        hop(1, 1)
        yield
        hop(0, 3)
        arrived("x2")
        hop(2, 1)
        yield
        for i, step in ((1, 2), (0, 4), (2, 2), (1, 3), (2, 3), (1, 4), (2, 4)):
            hop(i, step)
            yield
        for i in range(3):
            arrived(("x4", i))
        across_x(4)
        yield
        arrived("xc")

    gather_x = gather_blocks()
    next(gather_x)
    project(1)
    project(2)
    next(gather_x)
    for g in range(3, groups):
        project(g)

    def transposes(g):
        @pl.loop(0, 8)
        def _(p):
            st[8 * g + p] = s_sq[8 * g + p].T[0:R]

    def local(g, part):
        if part == 0:
            loads[2, g].wait()
            to_lines((v_raw,), g)

        @pl.loop(2 * part, 2 * part + 2)
        def _(i):
            for u in range(2):
                v_sq[u, 0:R, :] = natural(lines, 2 * i + u, u).astype(BF)
            for u in range(2):
                at = 8 * g + 2 * i + u
                base[at] = square(u) + dot(m_sq[at, 0:R, :], v_sq[u])

    def of_coupled(k, q):
        return gc[k // 16, k // 8 % 2, k // 4 % 2, q, k % 4].astype(F32)

    def of_exchange(k, q):
        d = (k // 16 + 4 - x) % 4
        return gx[jnp.where(d < 2, d, 5 - d), k // 8 % 2, k % 8, q].astype(F32)

    def both(of, at):
        k0, k1 = pairs[0, at], pairs[1, at]
        return jnp.concatenate([unpack(of(k0, q) + of(k1, q)) for q in range(4)], axis=0)

    def own_terms(g):
        @pl.loop(0, 4)
        def _(i):
            for u in range(2):
                at = 8 * g + 2 * i + u
                w_sq[u, 0:R, :] = both(of_exchange, at).astype(BF)
            for u in range(2):
                at = 8 * g + 2 * i + u
                pq[at] = dot(pq[at], w_sq[u]).astype(BF)

    early = [lambda g=g, part=part: local(g, part) for g in range(groups) for part in range(2)] + [lambda g=g: transposes(g) for g in range(groups)]
    late = [lambda g=g: own_terms(g) for g in range(groups)]

    def fill(work, count=1):
        for _ in range(count):
            if work:
                work.pop(0)()

    to_inv.wait()
    order = (2, 1, 3, 0)

    def ends(k, q):
        return pp[inv[0, k], q].astype(F32) + pp[inv[1, k], q].astype(F32)

    def each_a(q, c, put):
        @pl.loop(0, 4)
        def _(xx):
            for j in range(4):
                put(xx, q, j, ends(xx * 16 + c * 8 + j, q))

    def each_b(xx, c, put):
        @pl.loop(0, 4)
        def _(q):
            for j in range(4):
                put(q, xx, j, ends(xx * 16 + c * 8 + 4 + j, q))

    def put_in(ref, also=None):
        def put(t1, t2, j, value):
            if also is not None:
                value = value + also[t1, t2, j].astype(F32)
            ref[t1, t2, j] = value.astype(BF)

        return put

    for d in order:
        at = (y + d) % 4
        each_a(at, 1 - c, put_in(sb_a))
        send(sb_a.at[:, at], rc_a.at[:, at], "gx_1", 1 - c, "core", ("a", d))
        at = (x + d) % 4
        each_b(at, 1 - c, put_in(sb_b))
        send(sb_b.at[:, at], rc_b.at[:, at], "gx_1", 1 - c, "core", ("b", d))
    next(gather_x)

    def ready_a(d):
        arrived(("a", d))
        each_a((y + d) % 4, c, put_in(acc_a, rc_a))

    def ready_b(d):
        arrived(("b", d))
        each_b((x + d) % 4, c, put_in(acc_b, rc_b))

    def add(dst, *srcs):
        for j in range(dst.shape[0]):
            value = dst[j].astype(F32)
            for src in srcs:
                value = value + src[j].astype(F32)
            dst[j] = value.astype(BF)

    class Reduce:
        def __init__(self, name, axis1, p1, axis2, p2, acc, tr1, rx1, tr2, rx2, ready):
            self.name, self.axis1, self.p1, self.axis2, self.p2 = name, axis1, p1, axis2, p2
            self.acc, self.tr1, self.rx1, self.tr2, self.rx2, self.ready = acc, tr1, rx1, tr2, rx2, ready

        def sub(self, d1, d2):
            return self.acc.at[(self.p1 + d1) % 4, (self.p2 + d2) % 4]

        def first(self, turn, src, dst, *into):
            send(src, dst, self.axis1, (self.p1 + turn) % 4, "ring1", (self.name, *into))

        def second(self, turn, src, dst, *into):
            send(src, dst, self.axis2, (self.p2 + turn) % 4, "ring2", (self.name, *into))

        def s1(self, d):
            self.ready(d)
            k = order.index(d)
            self.first(1, self.sub(2, d).at[0:2], self.tr1.at[0, k], "u", d)
            self.first(3, self.sub(2, d).at[2:4], self.tr1.at[1, k], "d", d)
            self.first(1, self.sub(1, d).at[2:4], self.rx1.at[0, k, 2:4], "r", d)
            self.first(3, self.sub(3, d).at[0:2], self.rx1.at[1, k, 0:2], "r", d)

        def s2(self, d):
            k = order.index(d)
            arrived((self.name, "u", d))
            add(self.sub(1, d).at[0:2], self.tr1.at[0, k])
            self.first(1, self.sub(1, d).at[0:2], self.rx1.at[0, k, 0:2], "r", d)
            arrived((self.name, "d", d))
            add(self.sub(3, d).at[2:4], self.tr1.at[1, k])
            self.first(3, self.sub(3, d).at[2:4], self.rx1.at[1, k, 2:4], "r", d)

        def s3(self, d):
            k = order.index(d)
            arrived((self.name, "r", d))
            mine = self.sub(0, d)
            add(mine, self.rx1.at[0, k], self.rx1.at[1, k])
            if d == 2:
                self.second(1, mine.at[0:2], self.tr2.at[0], "u2")
                self.second(3, mine.at[2:4], self.tr2.at[1], "d2")
            if d == 1:
                self.second(1, mine.at[2:4], self.rx2.at[0, 2:4], "r2")
            if d == 3:
                self.second(3, mine.at[0:2], self.rx2.at[1, 0:2], "r2")

        def u3(self):
            arrived((self.name, "u2"))
            add(self.sub(0, 1).at[0:2], self.tr2.at[0])
            self.second(1, self.sub(0, 1).at[0:2], self.rx2.at[0, 0:2], "r2")
            arrived((self.name, "d2"))
            add(self.sub(0, 3).at[2:4], self.tr2.at[1])
            self.second(3, self.sub(0, 3).at[2:4], self.rx2.at[1, 2:4], "r2")

        def u4(self, at):
            arrived((self.name, "r2"))
            mine = self.sub(0, 0)
            for j in range(4):
                zb[at + j] = (mine[j].astype(F32) + self.rx2[0, j].astype(F32) + self.rx2[1, j].astype(F32)).astype(BF)

    both_rings = (
        Reduce("A", "gx_0", x, "gz", y, acc_a, tr_a, rx_a, tr_c, rx_c, ready_a),
        Reduce("B", "gz", y, "gx_0", x, acc_b, tr_b, rx_b, tr_d, rx_d, ready_b),
    )
    for d in order:
        for r in both_rings:
            r.s1(d)
    fill(early)
    next(gather_x)
    for i, d in enumerate(order):
        for r in both_rings:
            r.s2(d)
        if i < 3:
            fill(early)
            next(gather_x)
    for i, d in enumerate(order):
        for r in both_rings:
            r.s3(d)
        if i == 2:
            next(gather_x)
    for r in both_rings:
        r.u3()
    next(gather_x)
    for i, r in enumerate(both_rings):
        r.u4(4 * i)

    for d in (4, 3, 5, 2, 6, 1, 7):
        send(zb.at[(z + d) % 8], zr.at[d - 1], "gy", (z + d) % 8, "z", "z")
    fill(early, 1)
    next(gather_x)
    fill(early, 3)
    arrived("z")
    total = zb[z].astype(F32)
    for d in range(7):
        total = total + zr[d].astype(F32)
    domain = unpack(total).astype(BF)
    coupled = dot(domain, x_sq[...])
    gc[x, c, z // 4, y, z % 4] = pack(coupled).astype(BF)

    def across(ref):
        send(ref, ref, "gx_1", 1 - c, "over", "over")

    class Gather:
        def __init__(self, name, axis2, p2, axis3, p3, sub):
            self.name, self.axis2, self.p2, self.axis3, self.p3 = name, axis2, p2, axis3, p3
            self.at = sub

        def sub(self, d3, d2):
            return self.at((self.p3 + d3) % 4, (self.p2 + d2) % 4)

        def turn2(self, ref, d, *into):
            send(ref, ref, self.axis2, (self.p2 + d) % 4, "turn2", ("g" + self.name, *into))

        def turn3(self, ref, d, *into):
            send(ref, ref, self.axis3, (self.p3 + d) % 4, "turn3", ("g" + self.name, *into))

        def arrived(self, *into):
            arrived(("g" + self.name, *into))

        def spread(self, d):
            ref = self.sub(0, d)
            self.turn3(ref, 1, "u", d)
            self.turn3(ref, 3, "d", d)
            across(ref)

        def t0(self):
            ref = self.sub(0, 0)
            self.turn2(ref, 1, "u")
            self.turn2(ref, 3, "d")
            self.spread(0)

        def t1(self):
            self.arrived("u")
            self.turn2(self.sub(0, 3).at[0:2], 1, "far")
            self.arrived("d")
            self.turn2(self.sub(0, 1).at[2:4], 3, "far")
            self.spread(3)
            self.spread(1)

        def t3(self):
            self.arrived("far")
            self.spread(2)

        def on(self, d):
            self.arrived("u", d)
            ref = self.sub(3, d)
            self.turn3(ref.at[0:2], 1, "far", d)
            across(ref)
            self.arrived("d", d)
            ref = self.sub(1, d)
            self.turn3(ref.at[2:4], 3, "far", d)
            across(ref)

        def last(self, d):
            self.arrived("far", d)
            across(self.sub(2, d))

    own = gc.at[x, c, z // 4, y, z % 4]
    for d in (4, 3, 5, 2, 6, 1, 7):
        send(own, own, "gy", (z + d) % 8, "z", "gz")
    fill(early, 12)
    next(gather_x)
    arrived("gz")
    both_rings = (
        Gather("A", "gz", y, "gx_0", x, lambda i3, i2: gc.at[i3, c, 0, i2]),
        Gather("B", "gx_0", x, "gz", y, lambda i3, i2: gc.at[i2, c, 1, i3]),
    )
    for r in both_rings:
        r.t0()
    for _ in gather_x:
        pass
    fill(late)
    for r in both_rings:
        r.t1()
    for r in both_rings:
        r.on(0)
    for r in both_rings:
        r.t3()
    fill(late)
    for d in (3, 1):
        for r in both_rings:
            r.on(d)
    for r in both_rings:
        r.last(0)
    fill(late)
    for r in both_rings:
        r.on(2)
    fill(late)
    for d in (3, 1, 2):
        for r in both_rings:
            r.last(d)
    arrived("over")

    stores = []
    for g in range(groups):
        @pl.loop(0, 8 // UNROLL)
        def _(i):
            def right(u):
                at = 8 * g + UNROLL * i + u
                combined = (both(of_coupled, at) - pq[at].astype(F32)).astype(BF)
                w_sq[u, 0:R, :] = dot(combined, s_sq[at]).astype(BF)

            def left(u):
                at = 8 * g + UNROLL * i + u
                result = jnp.where(far < (ranks[at] + 1) * RSTEP, base[at] + dot(st[at], w_sq[u]), 0.0)
                tmp[u, 0] = result[:, 0:128]
                tmp[u, 1] = result[:, 128:256]

            def flat(u):
                p = UNROLL * i + u
                low = low_lanes(96)
                el, er, ol, oh = (tmp[u, j, pl.ds(e, 96, stride=2), :] for e in range(2) for j in range(2))
                ol, oh = pltpu.roll(ol, 64, 1), pltpu.roll(oh, 64, 1)
                lines[pl.ds(p, 96, stride=24), :] = el
                lines[pl.ds(8 + p, 96, stride=24), :] = jnp.where(low, er, ol)
                lines[pl.ds(16 + p, 96, stride=24), :] = jnp.where(low, ol, oh)

            skewed(UNROLL, right, left, flat)

        @pl.loop(0, LINES // 12)
        def _(i):
            for u in range(12):
                at = i * 12 + u
                s_raw[8 * g : 8 * g + 8, pl.ds(pl.multiple_of(at * 128, 128), 128)] = lines[
                    pl.ds(pl.multiple_of(at * 8, 8), 8), :
                ].astype(BF)

        copy = pltpu.make_async_copy(s_raw.at[8 * g : 8 * g + 8], o_ref.at[8 * g : 8 * g + 8], store_sem.at[g])
        copy.start()
        stores.append(copy)

    for copy in stores:
        copy.wait()
    assert len(leaving) == OUT and len(arriving) == INTO
    for index, size in leaving.values():
        await_all(send_sem.at[index], size)


def body(pair_list, rank_bucket, amplitudes, intersects, integrals, exchange_blocks):
    n = amplitudes.shape[0]
    hbm = pl.BlockSpec(memory_space=pl.ANY)
    tail = (CH, 128)
    return pl.pallas_call(
        kernel,
        in_specs=[hbm] * 6,
        out_specs=hbm,
        out_shape=jax.ShapeDtypeStruct((n, R * R), BF),
        scratch_shapes=[
            *[pltpu.VMEM((n, R * R), BF)] * 3,
            pltpu.VMEM((1, R * R), BF),
            *[pltpu.VMEM((LINES * 8, 128), F32)] * 2,
            pltpu.VMEM((LINES, 128), F32),
            pltpu.VMEM((UNROLL, 2, R, 128), F32),
            pltpu.VMEM((n, W, W), BF),
            pltpu.VMEM((n, W, W), BF),
            pltpu.VMEM((2, W, W), BF),
            pltpu.VMEM((W, W), BF),
            pltpu.VMEM((UNROLL, W, W), BF),
            pltpu.VMEM((n, R, W), BF),
            pltpu.VMEM((n, R, W), BF),
            pltpu.VMEM((n, R, W), F32),
            pltpu.VMEM((n + 1, 4) + tail, BF),
            pltpu.VMEM((4, 2, 2, 4, 4) + tail, BF),
            pltpu.VMEM((4, 2, 8, 4) + tail, BF),
            *[pltpu.VMEM((4, 4, 4) + tail, BF)] * 6,
            *[pltpu.VMEM((2, 4, 2) + tail, BF), pltpu.VMEM((2, 4, 4) + tail, BF)] * 2,
            *[pltpu.VMEM((2, 2) + tail, BF), pltpu.VMEM((2, 4) + tail, BF)] * 2,
            pltpu.VMEM((8,) + tail, BF),
            pltpu.VMEM((7,) + tail, BF),
            pltpu.VMEM((2, 128), jnp.int32),
            pltpu.SMEM((2, 128), jnp.int32),
            pltpu.SMEM((2, n), jnp.int32),
            pltpu.SMEM((n,), jnp.int32),
            pltpu.SemaphoreType.DMA((3, n // 8)),
            pltpu.SemaphoreType.DMA((n // 8,)),
            pltpu.SemaphoreType.DMA((4,)),
            pltpu.SemaphoreType.DMA((OUT,)),
            pltpu.SemaphoreType.DMA((INTO,)),
        ],
        compiler_params=pltpu.CompilerParams(collective_id=0, has_side_effects=True, vmem_limit_bytes=58 * 2**20),
    )(pair_list.T, rank_bucket, amplitudes, intersects, integrals, exchange_blocks)


def solution(mesh):
    torus = Mesh(mesh.devices.reshape(4, 2, mesh.shape["gy"], mesh.shape["gz"]), GX_GY_GZ)
    return jax.shard_map(
        body,
        mesh=torus,
        in_specs=(
            P(GX_GY_GZ, None),
            P(GX_GY_GZ),
            P(GX_GY_GZ, None),
            P(GX_GY_GZ, None),
            P(GX_GY_GZ, None),
            P(GX_GY, None),
        ),
        out_specs=P(GX_GY_GZ, None),
        check_vma=False,
    )
```

time: 364 us -> 79.6 us (0.22)
  waiting for transfers between devices: 245 us -> 0 us
  Pallas kernels: 0 us -> 76.3 us
  local copies, waits for them, and re-layouts: 61.2 us -> 3.22 us
  matrix products: 35.7 us -> 0 us
  between operations: 13.3 us -> 0.01 us
  starting transfers between devices: 4.49 us -> 0 us
    reduce_scatter x2 -> x0, waiting for transfers between devices: 83.9 us -> none  [own_block(): blocks = lax.psum_scatter(blocks, axes[k], scatter_dimension=0, tiled=True)]
    all_gather x1 -> x0, waiting for transfers between devices: 81.1 us -> none  [side_by_side(): lax.all_gather(both, axis, axis=dim, tiled=True)]
    pallas_call x0 -> x1, Pallas kernels: none -> 76.3 us  [body(): pl.pallas_call(kernel, in_specs=[hbm] * 6, out_specs=hbm, out_shape=jax.S...]
    unnamed x5 -> x0, waiting for transfers between devices: 73.8 us -> none
    dot_general x6 -> x0, matrix products: 35.7 us -> none  [the longest x1 10.1 us: body(): jnp.einsum('pab,pebc->peac', projected, picked_blocks, preferred_element_...]
    reshape x7 -> x0, local copies, waits for them, and re-layouts: 27.8 us -> none  [the longest x1 6.19 us: body(): flat_projected = projected.reshape(pair_rows, rank_width * rank_width)]
    gather x2 -> x0, local copies, waits for them, and re-layouts: 12.8 us -> none  [the longest x1 6.39 us: body(): picked_coupled = every_coupled[pair_list]]
    slice x1 -> x0, local copies, waits for them, and re-layouts: 12 us -> none  [side_by_side(): lax.slice_in_dim(whole, at, at + a.shape[along], axis=along)]
  transfers between devices with their start and end apart: 5 -> 0, of which waited for: 5 -> 0; matrix products, arithmetic and copies ran while one was open for 2% -> 0% of each run, Pallas kernels for 0% -> 0%
where the time goes in v3:
time: 79.6 us; the launch traced here: 79.5 us
  Pallas kernels  76.3 us (96%)
  local copies, waits for them, and re-layouts  3.22 us (4%)
    pallas_call x1, Pallas kernels, body(): pl.pallas_call(kernel, in_specs=[hbm] * 6, out_specs=hbm, out_shape=jax.S...  76.3 us
    unnamed x1, local copies, waits for them, and re-layouts  3.22 us

profile of v3, /device:TPU:1, one launch (start us, length us, event | category | flops | bytes accessed | tf_op | source)
XLA Modules:
  0.0 79.5 jit_solution(17617785728908589284)
XLA Ops:
  0.0 76.3 %shard_map.64 = bf16[32,36864]{1,0:T(8,128)(2,1)} custom-call(s32[2,32]{1,0:T(2,128)} %bitcast.1, s32[32]{0:T(128)} %ranks_hbm.1, bf16[32,36864]{1,0:T(8,128)(2,1)} %t_hbm.1, bf16[32,36864]{1,0:T(8,128)(2,1)} %s_hbm.1, bf16[32,36864]{1,0:T(8,128)(2,1)} %v_hbm.1, bf16[1,36864]{1,0:T(2,128)(2,1)} %x_hbm.1), custom_call_target="tpu_custom_call" | custom-call | tf_op jit(solution)/shard_map/pallas_call | solution.py:617
  76.3 3.2 %copy.8 = bf16[32,36864]{1,0:T(8,128)(2,1)} copy(bf16[32,36864]{1,0:T(8,128)(2,1)} %shard_map.64) | data formatting | bytes 4718592

commit v4 on v3

--- a/solution.py
+++ b/solution.py
@@ -15,7 +15,7 @@
 Q = 48
 CH = 72
 LINES = R * R // 128
-UNROLL = 4
+UNROLL = 8
 OUT, INTO = 11, 96
 GX_GY = ("gx_0", "gx_1", "gy")
 GX_GY_GZ = ("gx_0", "gx_1", "gy", "gz")
@@ -50,9 +50,9 @@
 
 def kernel(
     pairs_hbm, ranks_hbm, t_hbm, s_hbm, v_hbm, x_hbm, o_ref,
-    s_raw, t_raw, v_raw, x_raw, lines, lines2, xl, tmp, s_sq, m_sq, v_sq, x_sq, w_sq, st, pq, base, pp,
+    s_raw, t_raw, x_raw, lines, lines2, xl, tmp, s_sq, m_sq, v_sq, x_sq, w_sq, pq, base, pp,
     gc, gx, sb_a, sb_b, rc_a, rc_b, acc_a, acc_b, tr_a, rx_a, tr_b, rx_b, tr_c, rx_c, tr_d, rx_d, zb, zr,
-    inv_v, inv, pairs, ranks, load_sem, store_sem, small_sem, send_sem, recv_sem,
+    inv_v, inv, pairs, ranks, load_sem, small_sem, send_sem, recv_sem,
 ):
     n = s_raw.shape[0]
     groups = n // 8
@@ -71,11 +71,15 @@
         copy.start()
         small.append(copy)
     loads = {}
-    for i, g in [(i, g) for g in range(groups) for i in (0, 1)] + [(2, g) for g in range(groups)]:
-        src, dst = ((s_hbm, s_raw), (t_hbm, t_raw), (v_hbm, v_raw))[i]
+    def load(i, g):
+        src, dst = ((s_hbm, s_raw), (t_hbm, t_raw), (v_hbm, s_raw))[i]
         copy = pltpu.make_async_copy(src.at[8 * g : 8 * g + 8], dst.at[8 * g : 8 * g + 8], load_sem.at[i, g])
         copy.start()
         loads[i, g] = copy
+
+    for g in range(groups):
+        load(0, g)
+        load(1, g)
 
     leaving, arriving = {}, {}
 
@@ -111,10 +115,10 @@
         await_all(recv_sem.at[arriving[into][0]], arriving[into][1])
 
     def to_lines(raws, g):
-        @pl.loop(0, LINES // 12)
+        @pl.loop(0, LINES // 36)
         def _(i):
-            for u in range(12):
-                at = i * 12 + u
+            for u in range(36):
+                at = i * 36 + u
                 for raw, to in zip(raws, (lines, lines2)):
                     to[pl.ds(pl.multiple_of(at * 8, 8), 8), :] = raw[
                         8 * g : 8 * g + 8, pl.ds(pl.multiple_of(at * 128, 128), 128)
@@ -146,6 +150,9 @@
         loads[0, g].wait()
         loads[1, g].wait()
         to_lines((s_raw, t_raw), g)
+        load(2, g)
+        if g == 0:
+            small[0].wait()
 
         @pl.loop(0, 8 // UNROLL)
         def _(i):
@@ -174,7 +181,6 @@
 
             skewed(UNROLL, reshaped, left, right)
 
-    small[0].wait()
     project(0)
 
     small[2].wait()
@@ -273,19 +279,19 @@
     next(gather_x)
     project(1)
     project(2)
-    next(gather_x)
     for g in range(3, groups):
         project(g)
+    next(gather_x)
 
     def transposes(g):
         @pl.loop(0, 8)
         def _(p):
-            st[8 * g + p] = s_sq[8 * g + p].T[0:R]
+            m_sq[8 * g + p, 0:R, :] = s_sq[8 * g + p].T[0:R]
 
     def local(g, part):
         if part == 0:
             loads[2, g].wait()
-            to_lines((v_raw,), g)
+            to_lines((s_raw,), g)
 
         @pl.loop(2 * part, 2 * part + 2)
         def _(i):
@@ -357,7 +363,6 @@
         at = (x + d) % 4
         each_b(at, 1 - c, put_in(sb_b))
         send(sb_b.at[:, at], rc_b.at[:, at], "gx_1", 1 - c, "core", ("b", d))
-    next(gather_x)
 
     def ready_a(d):
         arrived(("a", d))
@@ -436,31 +441,39 @@
         Reduce("A", "gx_0", x, "gz", y, acc_a, tr_a, rx_a, tr_c, rx_c, ready_a),
         Reduce("B", "gz", y, "gx_0", x, acc_b, tr_b, rx_b, tr_d, rx_d, ready_b),
     )
-    for d in order:
+    def each(method, d):
         for r in both_rings:
-            r.s1(d)
+            getattr(r, method)(d)
+
+    each("s1", 2)
+    each("s1", 1)
     fill(early)
     next(gather_x)
-    for i, d in enumerate(order):
-        for r in both_rings:
-            r.s2(d)
-        if i < 3:
-            fill(early)
-            next(gather_x)
-    for i, d in enumerate(order):
-        for r in both_rings:
-            r.s3(d)
-        if i == 2:
-            next(gather_x)
+    each("s2", 2)
+    each("s1", 3)
+    next(gather_x)
+    each("s2", 1)
+    each("s1", 0)
+    fill(early)
+    next(gather_x)
+    each("s2", 3)
+    next(gather_x)
+    fill(early)
+    each("s2", 0)
+    each("s3", 2)
+    next(gather_x)
+    for d in (1, 3, 0):
+        each("s3", d)
     for r in both_rings:
         r.u3()
     next(gather_x)
+    fill(early)
     for i, r in enumerate(both_rings):
         r.u4(4 * i)
 
     for d in (4, 3, 5, 2, 6, 1, 7):
         send(zb.at[(z + d) % 8], zr.at[d - 1], "gy", (z + d) % 8, "z", "z")
-    fill(early, 1)
+    fill(early)
     next(gather_x)
     fill(early, 3)
     arrived("z")
@@ -501,15 +514,12 @@
             ref = self.sub(0, 0)
             self.turn2(ref, 1, "u")
             self.turn2(ref, 3, "d")
-            self.spread(0)
 
         def t1(self):
             self.arrived("u")
             self.turn2(self.sub(0, 3).at[0:2], 1, "far")
             self.arrived("d")
             self.turn2(self.sub(0, 1).at[2:4], 3, "far")
-            self.spread(3)
-            self.spread(1)
 
         def t3(self):
             self.arrived("far")
@@ -541,13 +551,18 @@
     )
     for r in both_rings:
         r.t0()
+    for r in both_rings:
+        r.spread(0)
+    for r in both_rings:
+        r.t1()
+    for d in (3, 1):
+        for r in both_rings:
+            r.spread(d)
+    for r in both_rings:
+        r.on(0)
     for _ in gather_x:
         pass
     fill(late)
-    for r in both_rings:
-        r.t1()
-    for r in both_rings:
-        r.on(0)
     for r in both_rings:
         r.t3()
     fill(late)
@@ -565,7 +580,6 @@
             r.last(d)
     arrived("over")
 
-    stores = []
     for g in range(groups):
         @pl.loop(0, 8 // UNROLL)
         def _(i):
@@ -576,7 +590,7 @@
 
             def left(u):
                 at = 8 * g + UNROLL * i + u
-                result = jnp.where(far < (ranks[at] + 1) * RSTEP, base[at] + dot(st[at], w_sq[u]), 0.0)
+                result = jnp.where(far < (ranks[at] + 1) * RSTEP, base[at] + dot(m_sq[at, 0:R, :], w_sq[u]), 0.0)
                 tmp[u, 0] = result[:, 0:128]
                 tmp[u, 1] = result[:, 128:256]
 
@@ -591,36 +605,45 @@
 
             skewed(UNROLL, right, left, flat)
 
-        @pl.loop(0, LINES // 12)
+        @pl.loop(0, LINES // 36)
         def _(i):
-            for u in range(12):
-                at = i * 12 + u
-                s_raw[8 * g : 8 * g + 8, pl.ds(pl.multiple_of(at * 128, 128), 128)] = lines[
+            for u in range(36):
+                at = i * 36 + u
+                o_ref[8 * g : 8 * g + 8, pl.ds(pl.multiple_of(at * 128, 128), 128)] = lines[
                     pl.ds(pl.multiple_of(at * 8, 8), 8), :
                 ].astype(BF)
 
-        copy = pltpu.make_async_copy(s_raw.at[8 * g : 8 * g + 8], o_ref.at[8 * g : 8 * g + 8], store_sem.at[g])
-        copy.start()
-        stores.append(copy)
-
-    for copy in stores:
-        copy.wait()
     assert len(leaving) == OUT and len(arriving) == INTO
     for index, size in leaving.values():
         await_all(send_sem.at[index], size)
 
 
+def store_kernel(r_ref, o_hbm, sem):
+    copies = []
+    for g in range(r_ref.shape[0] // 8):
+        copy = pltpu.make_async_copy(r_ref.at[8 * g : 8 * g + 8], o_hbm.at[8 * g : 8 * g + 8], sem.at[g])
+        copy.start()
+        copies.append(copy)
+    for copy in copies:
+        copy.wait()
+
+
 def body(pair_list, rank_bucket, amplitudes, intersects, integrals, exchange_blocks):
     n = amplitudes.shape[0]
     hbm = pl.BlockSpec(memory_space=pl.ANY)
+
+    def held(array):
+        return pltpu.with_memory_space_constraint(array, pltpu.HBM)
+
+    vmem = pl.BlockSpec(memory_space=pltpu.VMEM)
     tail = (CH, 128)
-    return pl.pallas_call(
+    residuals = pl.pallas_call(
         kernel,
         in_specs=[hbm] * 6,
-        out_specs=hbm,
+        out_specs=vmem,
         out_shape=jax.ShapeDtypeStruct((n, R * R), BF),
         scratch_shapes=[
-            *[pltpu.VMEM((n, R * R), BF)] * 3,
+            *[pltpu.VMEM((n, R * R), BF)] * 2,
             pltpu.VMEM((1, R * R), BF),
             *[pltpu.VMEM((LINES * 8, 128), F32)] * 2,
             pltpu.VMEM((LINES, 128), F32),
@@ -630,7 +653,6 @@
             pltpu.VMEM((2, W, W), BF),
             pltpu.VMEM((W, W), BF),
             pltpu.VMEM((UNROLL, W, W), BF),
-            pltpu.VMEM((n, R, W), BF),
             pltpu.VMEM((n, R, W), BF),
             pltpu.VMEM((n, R, W), F32),
             pltpu.VMEM((n + 1, 4) + tail, BF),
@@ -646,13 +668,20 @@
             pltpu.SMEM((2, n), jnp.int32),
             pltpu.SMEM((n,), jnp.int32),
             pltpu.SemaphoreType.DMA((3, n // 8)),
-            pltpu.SemaphoreType.DMA((n // 8,)),
             pltpu.SemaphoreType.DMA((4,)),
             pltpu.SemaphoreType.DMA((OUT,)),
             pltpu.SemaphoreType.DMA((INTO,)),
         ],
-        compiler_params=pltpu.CompilerParams(collective_id=0, has_side_effects=True, vmem_limit_bytes=58 * 2**20),
-    )(pair_list.T, rank_bucket, amplitudes, intersects, integrals, exchange_blocks)
+        compiler_params=pltpu.CompilerParams(collective_id=0, has_side_effects=True, vmem_limit_bytes=50 * 2**20),
+    )(held(pair_list.T), held(rank_bucket), amplitudes, intersects, integrals, held(exchange_blocks))
+    return pl.pallas_call(
+        store_kernel,
+        in_specs=[vmem],
+        out_specs=hbm,
+        out_shape=jax.ShapeDtypeStruct((n, R * R), BF),
+        scratch_shapes=[pltpu.SemaphoreType.DMA((n // 8,))],
+        compiler_params=pltpu.CompilerParams(vmem_limit_bytes=4 * 2**20),
+    )(residuals)
 
 
 def solution(mesh):

time: 79.6 us -> 71.9 us (0.903)
  Pallas kernels: 76.3 us -> 71.9 us
  local copies, waits for them, and re-layouts: 3.22 us -> 0 us
    pallas_call x1 -> x2, Pallas kernels: 76.3 us -> 71.9 us  [the longest x1 70.4 us: body(): pl.pallas_call(kernel, in_specs=[hbm] * 6, out_specs=vmem, out_shape=jax....]
    unnamed x1 -> x0, local copies, waits for them, and re-layouts: 3.22 us -> none
where the time goes in v4:
time: 71.9 us
  Pallas kernels  71.9 us (100%)
    pallas_call x1, Pallas kernels, body(): pl.pallas_call(kernel, in_specs=[hbm] * 6, out_specs=vmem, out_shape=jax....  70.4 us

profile of v4, /device:TPU:1, one launch (start us, length us, event | category | flops | bytes accessed | tf_op | source)
XLA Modules:
  0.0 71.9 jit_solution(13864355199486437798)
XLA Ops:
  0.0 70.4 %shard_map.64.r_ref = bf16[32,36864]{1,0:T(8,128)(2,1)S(1)} custom-call(s32[2,32]{1,0:T(2,128)} %bitcast.1, s32[32]{0:T(128)} %ranks_hbm.1, bf16[32,36864]{1,0:T(8,128)(2,1)} %t_hbm.1, bf16[32,36864]{1,0:T(8,128)(2,1)} %s_hbm.1, bf16[32,36864]{1,0:T(8,128)(2,1)} %v_hbm.1, bf16[1,36864]{1,0:T(2,128)(2,1)} %x_hbm.1), custom_call_target="tpu_custom_call" | custom-call | tf_op jit(solution)/shard_map/pallas_call | solution.py:640
  70.4 1.4 %shard_map.65 = bf16[32,36864]{1,0:T(8,128)(2,1)} custom-call(bf16[32,36864]{1,0:T(8,128)(2,1)S(1)} %shard_map.64.r_ref), custom_call_target="tpu_custom_call" | custom-call | tf_op jit(solution)/shard_map/pallas_call | solution.py:677
